TPU v7x, 128 devices: a whole 4x4x4 slice. The times are simulated.
128 devices in a mesh: grp: 32 (over y, z_hi, x), sub: 4 (over z_lo, core).
Axes of the slice: x: 4, y: 4, z: 4 (z_hi: 2, z_lo: 2; z = z_hi * 2 + z_lo), core: 2. Of those that a mesh axis runs over, the one named last changes fastest.
Arguments:
- master: float32 [16384, 3584], P(('grp', 'sub')), may hold values from -120 to 120
- moment_one: float32 [16384, 3584], P(('grp', 'sub')), may hold values from -6 to 6
- moment_two: float32 [16384, 3584], P(('grp', 'sub')), may hold values from 0.01 to 4
- gradient: float32 [16384, 3584], P(('grp', 'sub')), may hold values from -120 to 120
- partner: int32 [128], replicated, may hold values from 0 to 127, each once
- tensor_of_row: int32 [16384], replicated, may hold values from 0 to 7, never falling along the last dimension, each value on 1 to 4096 neighbouring positions
Outputs:
- new_master: float32 [16384, 3584], P(('grp', 'sub'))
- new_moment_one: float32 [16384, 3584], P(('grp', 'sub'))
- new_moment_two: float32 [16384, 3584], P(('grp', 'sub'))
Inputs may be any that keep to these rules, and one draw needn't show every extreme that they name: partner[n] is the device of new rank n; every device holds exactly one rank. `tensor_of_row`: tensor numbers never fall along the rows; each of the 8 tensors has one or more rows.
All inputs are finite; a program needn't handle non-finite values.
Results may differ from a plain program's by a relative error of at most 0.00007.
Values sent between devices are 32-bit elements; how exact they have to be, the bound alone decides.
No kernel may reach another device: no remote copies, remote signals or barrier semaphores. Data moves between devices by JAX's collectives and lax.ppermute only.
A program may use at most 128 MiB of HBM per device.

v0:
```python
import functools

import jax
import jax.numpy as jnp
from jax import lax
from jax.sharding import Mesh
from jax.sharding import PartitionSpec as P

LAYERS = 8
GRP_SUB = ("grp_0", "grp_1", "grp_2", "sub_0", "sub_1")


beta_one = 0.9
beta_two = 0.999
step_count = 10
adam_eps = 1e-06
trust_eps = 1e-06
learn_rate = 0.05
decay_rate = 0.01


def one_axis_at_a_time(x, axes):
    return functools.reduce(lax.psum, axes, x)


def tensor_totals(values, onehot):
    return jnp.dot(values[None, :], onehot, precision=lax.Precision.HIGHEST)[0]


def local(master, moment_one, moment_two, gradient, partner, tensor_of_row):
    rows_dev, width = master.shape
    devices = lax.axis_size(GRP_SUB)
    block = rows_dev // devices
    device_id = lax.axis_index(GRP_SUB)
    numbers = jnp.arange(devices, dtype=jnp.int32)
    matches = partner[None, :] == numbers[:, None]
    inverse = jnp.sum(jnp.where(matches, numbers[None, :], 0), axis=1)
    my_rank = lax.dynamic_index_in_dim(inverse, device_id, 0, keepdims=False)
    layer_ids = jnp.arange(LAYERS, dtype=jnp.int32)
    id_grid = tensor_of_row.reshape(devices, devices, block)
    new_ids = lax.dynamic_index_in_dim(id_grid, my_rank, 1, keepdims=False).reshape(rows_dev)
    new_hot = (new_ids[:, None] == layer_ids[None, :]).astype(jnp.float32)

    def outbound(values):
        return jnp.take(values.reshape(devices, block, width), inverse, axis=0)

    sending = (outbound(master), outbound(moment_one), outbound(moment_two))
    arrived = (
        lax.all_to_all(sending[0], GRP_SUB, split_axis=0, concat_axis=0, tiled=True),
        lax.all_to_all(sending[1], GRP_SUB, split_axis=0, concat_axis=0, tiled=True),
        lax.all_to_all(sending[2], GRP_SUB, split_axis=0, concat_axis=0, tiled=True),
    )
    weights, moment_old, square_old = [piece.reshape(rows_dev, width) for piece in arrived]
    first = beta_one * moment_old + (1.0 - beta_one) * gradient
    second = beta_two * square_old + (1.0 - beta_two) * gradient * gradient
    correct_one = 1.0 - beta_one**step_count
    correct_two = 1.0 - beta_two**step_count
    update = (
        first / correct_one / (jnp.sqrt(second / correct_two) + adam_eps) + decay_rate * weights
    )
    update_local = tensor_totals(jnp.sum(update * update, axis=1), new_hot)
    weight_local = tensor_totals(jnp.sum(weights * weights, axis=1), new_hot)
    weight_sq, update_sq = (
        one_axis_at_a_time(weight_local, GRP_SUB),
        one_axis_at_a_time(update_local, GRP_SUB),
    )
    ratio = jnp.sqrt(weight_sq) / (jnp.sqrt(update_sq) + trust_eps)
    row_ratio = jnp.dot(new_hot, ratio[:, None], precision=lax.Precision.HIGHEST)
    fresh = weights - learn_rate * row_ratio * update
    return (fresh, first, second)


def solution(mesh):
    finer = Mesh(mesh.devices.reshape(4, 2, 4, 2, 2), ("grp_0", "grp_1", "grp_2", "sub_0", "sub_1"))
    in_specs = (P(GRP_SUB, None), P(GRP_SUB, None), P(GRP_SUB, None), P(GRP_SUB, None), P(), P())
    out_specs = (P(GRP_SUB, None), P(GRP_SUB, None), P(GRP_SUB, None))
    return jax.shard_map(local, mesh=finer, in_specs=in_specs, out_specs=out_specs, check_vma=False)
```

profile of v0, /device:TPU:1, one launch (start us, length us, event | category | flops | bytes accessed | tf_op | source)
XLA Modules:
  0.0 169.4 jit_solution(15982042428079250486)
XLA Ops:
  0.6 0.0 copy-start
  0.6 0.9 select_reduce_fusion
  1.6 0.6 copy-done
  2.2 2.4 %gather_fusion.2 = f32[128,3584]{1,0:T(8,128)} fusion(f32[128,3584]{1,0:T(8,128)S(1)} %copy-done, s32[1024]{0:T(1024)S(1)} %pad_clamp_fusion), kind=kCustom, calls=%fused_computation.2.clone | custom fusion | bytes 3670528 | tf_op jit(solution)/shard_map/jit(_take)/gather | solution.py:45
  4.6 4.7 %gather_fusion.1 = f32[128,3584]{1,0:T(8,128)} fusion(f32[128,3584]{1,0:T(8,128)} %param.9, s32[1024]{0:T(1024)S(1)} %pad_clamp_fusion), kind=kCustom, calls=%fused_computation.1.clone | custom fusion | bytes 3670528 | tf_op jit(solution)/shard_map/jit(_take)/gather | solution.py:45
  9.2 4.7 %gather_fusion = f32[128,3584]{1,0:T(8,128)} fusion(f32[128,3584]{1,0:T(8,128)} %param.8, s32[1024]{0:T(1024)S(1)} %pad_clamp_fusion), kind=kCustom, calls=%fused_computation.clone | custom fusion | bytes 3670528 | tf_op jit(solution)/shard_map/jit(_take)/gather | solution.py:45
  13.9 5.0 %bitcast_select_fusion = (f32[128,1,3584]{2,0,1:T(8,128)S(1)}, f32[128,1,3584]{2,0,1:T(8,128)}, f32[128,1,3584]{2,0,1:T(8,128)}) fusion(f32[128,3584]{1,0:T(8,128)} %gather_fusion.2, pred[128]{0:T(512)(128)(4,1)S(1)} %compare_and_fusion, f32[128,3584]{1,0:T(8,128)} %gather_fusion.1, f32[128,3584]{1,0:T(8,128)} %gather_fusion), kind=kLoop, calls=%fused_computation.10 | loop fusion | flops 1376256 | bytes 11010176 | tf_op jit(solution)/shard_map/jit(_take)/select_n | solution.py:45
  18.9 3.1 %copy.17 = f32[128,1,3584]{2,1,0:T(1,128)} copy(f32[128,1,3584]{2,0,1:T(8,128)S(1)} %get-tuple-element.19) | data formatting | bytes 3670016 | tf_op jit(solution)/shard_map/jit(_take)/select_n | solution.py:45
  22.0 11.9 %all-to-all-start.2 = ((f32[128,1,3584]{2,1,0:T(1,128)}), f32[128,1,3584]{2,1,0:T(1,128)}, u32[]{:S(2)}, u32[]{:S(2)}) async-start(f32[128,1,3584]{2,1,0:T(1,128)} %copy.17), calls=%async_computation.2 | async-start | bytes 3670016 | tf_op jit(solution)/shard_map/all_to_all | solution.py:51
  33.9 4.6 %copy.15 = f32[128,1,3584]{2,1,0:T(1,128)} copy(f32[128,1,3584]{2,0,1:T(8,128)} %get-tuple-element.20) | data formatting | bytes 3670016 | tf_op jit(solution)/shard_map/jit(_take)/select_n | solution.py:45
  38.5 22.3 %all-to-all-done.2 = f32[128,1,3584]{2,1,0:T(1,128)} async-done(((f32[128,1,3584]{2,1,0:T(1,128)}), f32[128,1,3584]{2,1,0:T(1,128)}, u32[]{:S(2)}, u32[]{:S(2)}) %all-to-all-start.2) | async-done | bytes 1835040 | tf_op jit(solution)/shard_map/all_to_all | solution.py:51
  60.8 5.4 %all-to-all-start.1 = ((f32[128,1,3584]{2,1,0:T(1,128)}), f32[128,1,3584]{2,1,0:T(1,128)}, u32[]{:S(2)}, u32[]{:S(2)}) async-start(f32[128,1,3584]{2,1,0:T(1,128)} %copy.15), calls=%async_computation.1 | async-start | bytes 3670016 | tf_op jit(solution)/shard_map/all_to_all | solution.py:50
  66.3 4.6 %copy.14 = f32[128,1,3584]{2,1,0:T(1,128)} copy(f32[128,1,3584]{2,0,1:T(8,128)} %get-tuple-element.21) | data formatting | bytes 3670016 | tf_op jit(solution)/shard_map/jit(_take)/select_n | solution.py:45
  70.9 0.0 copy-start.1
  70.9 22.4 %all-to-all-done.1 = f32[128,1,3584]{2,1,0:T(1,128)} async-done(((f32[128,1,3584]{2,1,0:T(1,128)}), f32[128,1,3584]{2,1,0:T(1,128)}, u32[]{:S(2)}, u32[]{:S(2)}) %all-to-all-start.1) | async-done | bytes 1835040 | tf_op jit(solution)/shard_map/all_to_all | solution.py:50
  93.3 5.6 %all-to-all-start = ((f32[128,1,3584]{2,1,0:T(1,128)}), f32[128,1,3584]{2,1,0:T(1,128)}, u32[]{:S(2)}, u32[]{:S(2)}) async-start(f32[128,1,3584]{2,1,0:T(1,128)} %copy.14), calls=%async_computation | async-start | bytes 3670016 | tf_op jit(solution)/shard_map/all_to_all | solution.py:49
  99.0 0.6 dynamic_slice.8
  101.5 0.0 copy-done.1
  101.5 0.2 dynamic-slice_reduce_fusion
  101.7 24.3 %all-to-all-done = f32[128,1,3584]{2,1,0:T(1,128)} async-done(((f32[128,1,3584]{2,1,0:T(1,128)}), f32[128,1,3584]{2,1,0:T(1,128)}, u32[]{:S(2)}, u32[]{:S(2)}) %all-to-all-start) | async-done | bytes 1835040 | tf_op jit(solution)/shard_map/all_to_all | solution.py:49
  126.0 7.1 %multiply_reduce_fusion = (f32[128]{0:T(128)S(1)}, f32[128,3584]{1,0:T(8,128)}, f32[128,3584]{1,0:T(8,128)}, f32[128,3584]{1,0:T(8,128)}, f32[128]{0:T(128)S(1)}) fusion(f32[128,1,3584]{2,1,0:T(1,128)} %all-to-all-done, f32[128,3584]{1,0:T(8,128)} %param.11, f32[128,1,3584]{2,1,0:T(1,128)} %all-to-all-done.1, f32[128,1,3584]{2,1,0:T(1,128)} %all-to-all-done.2), kind=kLoop, calls=%fused_computation.16 | loop fusion | flops 7798528 | bytes 12846080 | tf_op jit(solution)/shard_map/reduce_sum | solution.py:61
  133.1 0.2 convolution_bitcast_fusion.1
  133.3 0.2 convolution_bitcast_fusion.2
  133.5 6.9 %all-reduce.1 = (f32[8]{0:T(128)S(1)}, f32[8]{0:T(128)S(1)}) all-reduce(f32[8]{0:T(128)S(1)} %convolution_bitcast_fusion.1, f32[8]{0:T(128)S(1)} %convolution_bitcast_fusion.2), channel_id=1, replica_groups=mesh['grp_0'=4,'grp_1'=2,'grp_2'=4,'sub_0'=2,'sub_1'=2] {'grp_0'}, use_global_device_ids=true, to_apply=%region_8.10 | all-reduce | flops 16 | bytes 128 | tf_op jit(solution)/shard_map/psum | solution.py:23
  140.4 5.3 %all-reduce.4 = (f32[8]{0:T(128)S(1)}, f32[8]{0:T(128)S(1)}) all-reduce(f32[8]{0:T(128)S(1)} %get-tuple-element.6, f32[8]{0:T(128)S(1)} %get-tuple-element.7), channel_id=1, replica_groups=mesh['grp_0'=4,'grp_1'=2,'grp_2'=4,'sub_0'=2,'sub_1'=2] {'grp_1'}, use_global_device_ids=true, to_apply=%region_9.11 | all-reduce | flops 16 | bytes 128 | tf_op jit(solution)/shard_map/psum | solution.py:23
  145.7 6.6 %all-reduce = (f32[8]{0:T(128)S(1)}, f32[8]{0:T(128)S(1)}) all-reduce(f32[8]{0:T(128)S(1)} %get-tuple-element.12, f32[8]{0:T(128)S(1)} %get-tuple-element.13), channel_id=1, replica_groups=mesh['grp_0'=4,'grp_1'=2,'grp_2'=4,'sub_0'=2,'sub_1'=2] {'grp_2'}, use_global_device_ids=true, to_apply=%region_10.12 | all-reduce | flops 16 | bytes 128 | tf_op jit(solution)/shard_map/psum | solution.py:23
  152.3 3.8 %all-reduce.3 = (f32[8]{0:T(128)S(1)}, f32[8]{0:T(128)S(1)}) all-reduce(f32[8]{0:T(128)S(1)} %get-tuple-element.4, f32[8]{0:T(128)S(1)} %get-tuple-element.5), channel_id=1, replica_groups=mesh['grp_0'=4,'grp_1'=2,'grp_2'=4,'sub_0'=2,'sub_1'=2] {'sub_0'}, use_global_device_ids=true, to_apply=%region_11.13 | all-reduce | flops 16 | bytes 128 | tf_op jit(solution)/shard_map/psum | solution.py:23
  156.1 9.5 %all-reduce.2 = (f32[8]{0:T(128)S(1)}, f32[8]{0:T(128)S(1)}) all-reduce(f32[8]{0:T(128)S(1)} %get-tuple-element.10, f32[8]{0:T(128)S(1)} %get-tuple-element.11), channel_id=1, replica_groups=mesh['grp_0'=4,'grp_1'=2,'grp_2'=4,'sub_0'=2,'sub_1'=2] {'sub_1'}, use_global_device_ids=true, to_apply=%region_12.14 | all-reduce | flops 16 | bytes 128 | tf_op jit(solution)/shard_map/psum | solution.py:23
  165.6 0.2 fusion.3
  165.8 3.6 %bitcast_subtract_fusion = f32[128,3584]{1,0:T(8,128)} fusion(f32[128,3584]{1,0:T(8,128)} %get-tuple-element.15, f32[128,1,3584]{2,1,0:T(1,128)} %all-to-all-done, f32[128]{0:T(128)S(1)} %fusion.3), kind=kLoop, calls=%fused_computation.5 | loop fusion | flops 917504 | bytes 5505536 | tf_op jit(solution)/shard_map/sub | solution.py:69
  (3 shorter events, 0.0 us)
Async XLA Ops:
  0.6 1.5 copy-start
  22.0 38.8 %all-to-all-start.2 = ((f32[128,1,3584]{2,1,0:T(1,128)}), f32[128,1,3584]{2,1,0:T(1,128)}, u32[]{:S(2)}, u32[]{:S(2)}) async-start(f32[128,1,3584]{2,1,0:T(1,128)} %copy.17), calls=%async_computation.2 | async-start | bytes 3670016 | tf_op jit(solution)/shard_map/all_to_all | solution.py:51
  60.8 32.5 %all-to-all-start.1 = ((f32[128,1,3584]{2,1,0:T(1,128)}), f32[128,1,3584]{2,1,0:T(1,128)}, u32[]{:S(2)}, u32[]{:S(2)}) async-start(f32[128,1,3584]{2,1,0:T(1,128)} %copy.15), calls=%async_computation.1 | async-start | bytes 3670016 | tf_op jit(solution)/shard_map/all_to_all | solution.py:50
  70.9 30.6 %copy-start.1 = (s32[16384]{0:T(1024)S(1)}, s32[16384]{0:T(1024)}, u32[]{:S(2)}) copy-start(s32[16384]{0:T(1024)} %param.13) | copy-start | bytes 196612
  93.3 32.7 %all-to-all-start = ((f32[128,1,3584]{2,1,0:T(1,128)}), f32[128,1,3584]{2,1,0:T(1,128)}, u32[]{:S(2)}, u32[]{:S(2)}) async-start(f32[128,1,3584]{2,1,0:T(1,128)} %copy.14), calls=%async_computation | async-start | bytes 3670016 | tf_op jit(solution)/shard_map/all_to_all | solution.py:49
where the time goes:
time: 170 us; the launch traced here: 169 us
  waiting for transfers between devices  69.1 us (41%)
  blocking collectives  32.1 us (19%)
  local copies, waits for them, and re-layouts  25.4 us (15%)
  starting transfers between devices  22.9 us (13%)
  other arithmetic  16.6 us (10%)
  between operations  2.67 us (2%)
    psum x5, blocking collectives, one_axis_at_a_time(): return functools.reduce(lax.psum, axes, x)  32.1 us
    all_to_all x1, waiting for transfers between devices, local(): lax.all_to_all(sending[0], GRP_SUB, split_axis=0, concat_axis=0, tiled=True)  24.3 us
    all_to_all x1, waiting for transfers between devices, local(): lax.all_to_all(sending[1], GRP_SUB, split_axis=0, concat_axis=0, tiled=True)  22.4 us
    all_to_all x1, waiting for transfers between devices, local(): lax.all_to_all(sending[2], GRP_SUB, split_axis=0, concat_axis=0, tiled=True)  22.3 us
    select_n x3, local copies, waits for them, and re-layouts, outbound(): return jnp.take(values.reshape(devices, block, width), inverse, axis=0)  12.3 us
    all_to_all x1, starting transfers between devices, local(): lax.all_to_all(sending[2], GRP_SUB, split_axis=0, concat_axis=0, tiled=True)  11.9 us
    gather x3, local copies, waits for them, and re-layouts, outbound(): return jnp.take(values.reshape(devices, block, width), inverse, axis=0)  11.8 us
    reduce_sum x1, other arithmetic, local(): update_local = tensor_totals(jnp.sum(update * update, axis=1), new_hot)  7.06 us
  transfers between devices with their start and end apart: 3, of which 3 were waited for; matrix products, arithmetic and copies ran while one was open for 6% of the time, Pallas kernels for 0%

commit v1 on v0

v1 whole, which is shorter than its diff:
```python
import functools

import jax
import jax.numpy as jnp
from jax import lax
from jax.experimental import pallas as pl
from jax.experimental.pallas import tpu as pltpu
from jax.sharding import Mesh
from jax.sharding import PartitionSpec as P

LAYERS = 8
GRP_SUB = ("grp", "sub")
LANES = 128
SUB = 8

beta_one = 0.9
beta_two = 0.999
step_count = 10
adam_eps = 1e-06
trust_eps = 1e-06
learn_rate = 0.05
decay_rate = 0.01
correct_one = 1.0 - beta_one**step_count
correct_two = 1.0 - beta_two**step_count


def pack_body(partner, master, one, two, out, lines, *, chunks, rows_step):
    pitch = 3 * chunks
    step = pl.program_id(0)

    def group(g, carry):
        for a, ref in enumerate((master, one, two)):
            for c in range(chunks):
                tile = ref[pl.ds(pl.multiple_of(g * SUB, SUB), SUB), c * LANES : (c + 1) * LANES]
                lines[pl.ds(a * chunks + c, SUB, stride=pitch), :] = tile
        for j in range(SUB):
            slot = partner[step * rows_step + g * SUB + j] * pitch
            for i in range(0, pitch, SUB):
                size = min(SUB, pitch - i)
                out[pl.ds(slot + i, size), :] = lines[j * pitch + i : j * pitch + i + size, :]
        return carry

    lax.fori_loop(0, rows_step // SUB, group, 0)


def adam_tiles(recv, grad, base, row, c, chunks):
    pitch = 3 * chunks
    weights = recv[pl.ds(base + c, SUB, stride=pitch), :]
    old_one = recv[pl.ds(base + chunks + c, SUB, stride=pitch), :]
    old_two = recv[pl.ds(base + 2 * chunks + c, SUB, stride=pitch), :]
    g = grad[pl.ds(row, SUB), c * LANES : (c + 1) * LANES]
    first = beta_one * old_one + (1.0 - beta_one) * g
    second = beta_two * old_two + (1.0 - beta_two) * g * g
    update = (first * (1.0 / correct_one)) / (
        jnp.sqrt(second * (1.0 / correct_two)) + adam_eps
    ) + decay_rate * weights
    return weights, first, second, update


def tensor_ids(ids, partner, device, row):
    mine = partner[...] == device
    return jnp.sum(jnp.where(mine, ids[pl.ds(row, SUB), :], 0), axis=1, keepdims=True)


def sums_body(device, partner, ids, recv, grad, out, acc, *, chunks, rows_step):
    pitch = 3 * chunks
    step = pl.program_id(0)

    @pl.when(step == 0)
    def _():
        acc[...] = jnp.zeros_like(acc)

    lane = lax.broadcasted_iota(jnp.int32, (SUB, LANES), 1)

    def group(g, carry):
        row = pl.multiple_of(g * SUB, SUB)
        update_sq = jnp.zeros((SUB, LANES), jnp.float32)
        weight_sq = jnp.zeros((SUB, LANES), jnp.float32)
        for c in range(chunks):
            weights, _, _, update = adam_tiles(recv, grad, g * SUB * pitch, row, c, chunks)
            update_sq += update * update
            weight_sq += weights * weights
        mine = tensor_ids(ids, partner, device[0], row)
        update_row = jnp.sum(update_sq, axis=1, keepdims=True)
        weight_row = jnp.sum(weight_sq, axis=1, keepdims=True)
        acc[...] += jnp.where(lane == mine, update_row, 0.0) + jnp.where(
            lane == mine + LAYERS, weight_row, 0.0
        )
        return carry

    lax.fori_loop(0, rows_step // SUB, group, 0)

    @pl.when(step == pl.num_programs(0) - 1)
    def _():
        total = jnp.sum(acc[...], axis=0, keepdims=True)
        out[...] = jnp.broadcast_to(total[None], out.shape)


def moments_body(recv, grad, first_out, second_out, update_out, weights_out, *, chunks, rows_step):
    pitch = 3 * chunks

    def group(g, carry):
        row = pl.multiple_of(g * SUB, SUB)
        for c in range(chunks):
            weights, first, second, update = adam_tiles(recv, grad, g * SUB * pitch, row, c, chunks)
            cols = slice(c * LANES, (c + 1) * LANES)
            first_out[pl.ds(row, SUB), cols] = first
            second_out[pl.ds(row, SUB), cols] = second
            update_out[pl.ds(row, SUB), cols] = update
            weights_out[pl.ds(row, SUB), cols] = weights
        return carry

    lax.fori_loop(0, rows_step // SUB, group, 0)


def master_body(device, partner, ids, sums, weights, update, out, *, chunks, rows_step):
    total = jnp.sum(sums[...], axis=0)
    update_sq = total
    weight_sq = pltpu.roll(jnp.broadcast_to(total, (SUB, LANES)), LANES - LAYERS, 1)[:1]
    ratio = jnp.sqrt(weight_sq) / (jnp.sqrt(update_sq) + trust_eps)
    lane = lax.broadcasted_iota(jnp.int32, (SUB, LANES), 1)

    def group(g, carry):
        row = pl.multiple_of(g * SUB, SUB)
        mine = tensor_ids(ids, partner, device[0], row)
        row_ratio = jnp.sum(jnp.where(lane == mine, ratio, 0.0), axis=1, keepdims=True)
        scale = learn_rate * row_ratio
        out[pl.ds(row, SUB), :] = weights[pl.ds(row, SUB), :] - scale * update[pl.ds(row, SUB), :]
        return carry

    lax.fori_loop(0, rows_step // SUB, group, 0)


def local(master, moment_one, moment_two, gradient, partner, tensor_of_row):
    rows, width = master.shape
    devices = lax.axis_size(GRP_SUB)
    chunks = width // LANES
    pitch = 3 * chunks
    steps = 4
    rows_step = rows // steps
    device = lax.axis_index(GRP_SUB).astype(jnp.int32).reshape(1)
    partner_row = partner.reshape(1, devices)
    ids = tensor_of_row.reshape(rows, devices)
    size = dict(chunks=chunks, rows_step=rows_step)
    row_spec = pl.BlockSpec((rows_step, width), lambda i: (i, 0))
    recv_spec = pl.BlockSpec((rows_step * pitch, LANES), lambda i: (i, 0))
    ids_spec = pl.BlockSpec((rows_step, devices), lambda i: (i, 0))
    whole = lambda *shape: pl.BlockSpec(shape, lambda i: (0,) * len(shape))
    scalars = pl.BlockSpec(memory_space=pltpu.SMEM)
    array = jax.ShapeDtypeStruct((rows, width), jnp.float32)

    packed = pl.pallas_call(
        functools.partial(pack_body, **size),
        grid=(steps,),
        in_specs=[scalars, row_spec, row_spec, row_spec],
        out_specs=whole(rows * pitch, LANES),
        out_shape=jax.ShapeDtypeStruct((rows * pitch, LANES), jnp.float32),
        scratch_shapes=[pltpu.VMEM((SUB * pitch, LANES), jnp.float32)],
        name="pack",
    )(partner, master, moment_one, moment_two)
    sent = packed.reshape(devices, 1, pitch * LANES)
    recv = lax.all_to_all(sent, GRP_SUB, split_axis=0, concat_axis=0, tiled=True)
    recv = recv.reshape(rows * pitch, LANES)

    sums = pl.pallas_call(
        functools.partial(sums_body, **size),
        grid=(steps,),
        in_specs=[scalars, whole(1, devices), ids_spec, recv_spec, row_spec],
        out_specs=whole(devices, 1, LANES),
        out_shape=jax.ShapeDtypeStruct((devices, 1, LANES), jnp.float32),
        scratch_shapes=[pltpu.VMEM((SUB, LANES), jnp.float32)],
        name="sums",
    )(device, partner_row, ids, recv, gradient)
    all_sums = lax.all_to_all(sums, GRP_SUB, split_axis=0, concat_axis=0, tiled=True)

    first, second, update, weights = pl.pallas_call(
        functools.partial(moments_body, **size),
        grid=(steps,),
        in_specs=[recv_spec, row_spec],
        out_specs=[row_spec] * 4,
        out_shape=[array] * 4,
        cost_estimate=pl.CostEstimate(flops=30_000_000, bytes_accessed=15_000_000, transcendentals=1_000_000),
        name="moments",
    )(recv, gradient)

    fresh = pl.pallas_call(
        functools.partial(master_body, **size),
        grid=(steps,),
        in_specs=[scalars, whole(1, devices), ids_spec, whole(devices, 1, LANES), row_spec, row_spec],
        out_specs=row_spec,
        out_shape=array,
        name="fresh",
    )(device, partner_row, ids, all_sums, weights, update)
    return (fresh, first, second)


def solution(mesh):
    rows = P(GRP_SUB, None)
    return jax.shard_map(
        local,
        mesh=mesh,
        in_specs=(rows, rows, rows, rows, P(), P()),
        out_specs=(rows, rows, rows),
        check_vma=False,
    )
```

time: 170 us -> 118 us (0.69)
  blocking collectives: 32.1 us -> 0 us
  Pallas kernels: 0 us -> 25.3 us
  local copies, waits for them, and re-layouts: 25.4 us -> 0.62 us
  other arithmetic: 16.6 us -> 0 us
  between operations: 2.67 us -> 0.66 us
    psum x5 -> x0, blocking collectives: 32.1 us -> none  [one_axis_at_a_time(): return functools.reduce(lax.psum, axes, x)]
    pallas_call x0 -> x4, Pallas kernels: none -> 25.3 us  [the longest x1 6.92 us: local(): pl.pallas_call(functools.partial(moments_body, **size), grid=(steps,), in...]
    select_n x3 -> x0, local copies, waits for them, and re-layouts: 12.3 us -> none  [outbound(): return jnp.take(values.reshape(devices, block, width), inverse, axis=0)]
    gather x3 -> x0, local copies, waits for them, and re-layouts: 11.8 us -> none  [outbound(): return jnp.take(values.reshape(devices, block, width), inverse, axis=0)]
    reduce_sum x2 -> x0, other arithmetic: 7.95 us -> none  [the longest x1 7.06 us: local(): update_local = tensor_totals(jnp.sum(update * update, axis=1), new_hot)]
    select_n x2 -> x0, other arithmetic: 4.99 us -> none  [outbound(): return jnp.take(values.reshape(devices, block, width), inverse, axis=0)]
    sub x1 -> x0, other arithmetic: 3.64 us -> none  [local(): fresh = weights - learn_rate * row_ratio * update]
    all_to_all x3 -> x2, starting transfers between devices: 22.9 us -> 22 us  [the longest x1 11.9 us: local(): lax.all_to_all(sent, GRP_SUB, split_axis=0, concat_axis=0, tiled=True)]
  transfers between devices with their start and end apart: 3 -> 2, of which waited for: 3 -> 2; matrix products, arithmetic and copies ran while one was open for 6% -> 0% of each run, Pallas kernels for 0% -> 6%
where the time goes in v1:
time: 118 us
  waiting for transfers between devices  69.4 us (59%)
  Pallas kernels  25.3 us (21%)
  starting transfers between devices  22 us (19%)
    all_to_all x1, waiting for transfers between devices, local(): lax.all_to_all(sent, GRP_SUB, split_axis=0, concat_axis=0, tiled=True)  66.5 us
    all_to_all x1, starting transfers between devices, local(): lax.all_to_all(sent, GRP_SUB, split_axis=0, concat_axis=0, tiled=True)  11.9 us
    all_to_all x1, starting transfers between devices, local(): lax.all_to_all(sums, GRP_SUB, split_axis=0, concat_axis=0, tiled=True)  10.1 us
    pallas_call x1, Pallas kernels, local(): pl.pallas_call(functools.partial(moments_body, **size), grid=(steps,), in...  6.92 us
    pallas_call x1, Pallas kernels, local(): pl.pallas_call(functools.partial(master_body, **size), grid=(steps,), in_...  6.25 us
    pallas_call x1, Pallas kernels, local(): pl.pallas_call(functools.partial(sums_body, **size), grid=(steps,), in_sp...  6.09 us
    pallas_call x1, Pallas kernels, local(): pl.pallas_call(functools.partial(pack_body, **size), grid=(steps,), in_sp...  6.02 us
    all_to_all x1, waiting for transfers between devices, local(): lax.all_to_all(sums, GRP_SUB, split_axis=0, concat_axis=0, tiled=True)  2.87 us
  transfers between devices with their start and end apart: 2, of which 2 were waited for; matrix products, arithmetic and copies ran while one was open for 0% of the time, Pallas kernels for 6%

profile of v1, /device:TPU:1, one launch (start us, length us, event | category | flops | bytes accessed | tf_op | source)
XLA Modules:
  0.0 117.9 jit_solution(2141589281968596981)
XLA Ops:
  0.6 6.0 %pack.1 = f32[10752,128]{1,0:T(8,128)} custom-call(s32[128]{0:T(128)} %partner.1, f32[128,3584]{1,0:T(8,128)} %master.1, f32[128,3584]{1,0:T(8,128)} %one.1, f32[128,3584]{1,0:T(8,128)} %two.1), custom_call_target="tpu_custom_call" | custom-call | tf_op jit(solution)/shard_map/pack/pallas_call | solution.py:152
  6.7 11.9 %all-to-all-start = ((f32[128,1,10752]{2,1,0:T(1,128)}), f32[128,1,10752]{2,1,0:T(1,128)}, u32[]{:S(2)}, u32[]{:S(2)}) async-start(f32[128,1,10752]{2,1,0:T(1,128)} %bitcast.5), calls=%async_computation | async-start | bytes 11010048 | tf_op jit(solution)/shard_map/all_to_all | solution.py:162
  18.6 66.5 %all-to-all-done = f32[128,1,10752]{2,1,0:T(1,128)} async-done(((f32[128,1,10752]{2,1,0:T(1,128)}), f32[128,1,10752]{2,1,0:T(1,128)}, u32[]{:S(2)}, u32[]{:S(2)}) %all-to-all-start) | async-done | bytes 5505056 | tf_op jit(solution)/shard_map/all_to_all | solution.py:162
  85.0 6.1 %sums.1 = f32[128,1,128]{2,1,0:T(1,128)} custom-call(s32[1]{0:T(128)} %bitcast.device, s32[1,128]{1,0:T(1,128)} %bitcast.8, s32[128,128]{1,0:T(8,128)} %bitcast.6, f32[10752,128]{1,0:T(8,128)} %bitcast.4.recv, f32[128,3584]{1,0:T(8,128)} %grad.3), custom_call_target="tpu_custom_call" | custom-call | tf_op jit(solution)/shard_map/sums/pallas_call | solution.py:165
  91.1 10.1 %all-to-all-start.1 = ((f32[128,1,128]{2,1,0:T(1,128)}), f32[128,1,128]{2,1,0:T(1,128)S(1)}, u32[]{:S(2)}, u32[]{:S(2)}) async-start(f32[128,1,128]{2,1,0:T(1,128)} %sums.1), calls=%async_computation.1 | async-start | bytes 131072 | tf_op jit(solution)/shard_map/all_to_all | solution.py:174
  101.3 6.9 %moments.1 = (f32[128,3584]{1,0:T(8,128)}, f32[128,3584]{1,0:T(8,128)}, f32[128,3584]{1,0:T(8,128)}, f32[128,3584]{1,0:T(8,128)}) custom-call(f32[10752,128]{1,0:T(8,128)} %bitcast.4.recv, f32[128,3584]{1,0:T(8,128)} %grad.3), custom_call_target="tpu_custom_call" | custom-call | flops 30000000 | bytes 15000000 | tf_op jit(solution)/shard_map/moments/pallas_call | solution.py:176
  108.2 2.9 %all-to-all-done.1.sums = f32[128,1,128]{2,1,0:T(1,128)S(1)} async-done(((f32[128,1,128]{2,1,0:T(1,128)}), f32[128,1,128]{2,1,0:T(1,128)S(1)}, u32[]{:S(2)}, u32[]{:S(2)}) %all-to-all-start.1) | async-done | bytes 65568 | tf_op jit(solution)/shard_map/all_to_all | solution.py:174
  111.1 0.0 copy-start
  111.1 0.6 copy-done
  111.7 6.3 %fresh.1 = f32[128,3584]{1,0:T(8,128)} custom-call(s32[1]{0:T(128)} %bitcast.device, s32[1,128]{1,0:T(1,128)} %bitcast.9, s32[128,128]{1,0:T(8,128)} %bitcast.7, f32[128,1,128]{2,1,0:T(1,128)} %copy-done, f32[128,3584]{1,0:T(8,128)} %get-tuple-element.7.weights, f32[128,3584]{1,0:T(8,128)} %get-tuple-element.8.update), custom_call_target="tpu_custom_call" | custom-call | tf_op jit(solution)/shard_map/fresh/pallas_call | solution.py:186
Async XLA Ops:
  6.7 78.4 %all-to-all-start = ((f32[128,1,10752]{2,1,0:T(1,128)}), f32[128,1,10752]{2,1,0:T(1,128)}, u32[]{:S(2)}, u32[]{:S(2)}) async-start(f32[128,1,10752]{2,1,0:T(1,128)} %bitcast.5), calls=%async_computation | async-start | bytes 11010048 | tf_op jit(solution)/shard_map/all_to_all | solution.py:162
  91.1 19.9 %all-to-all-start.1 = ((f32[128,1,128]{2,1,0:T(1,128)}), f32[128,1,128]{2,1,0:T(1,128)S(1)}, u32[]{:S(2)}, u32[]{:S(2)}) async-start(f32[128,1,128]{2,1,0:T(1,128)} %sums.1), calls=%async_computation.1 | async-start | bytes 131072 | tf_op jit(solution)/shard_map/all_to_all | solution.py:174
  111.1 0.6 copy-start

commit v2 on v1

--- a/solution.py
+++ b/solution.py
@@ -24,23 +24,37 @@
 correct_two = 1.0 - beta_two**step_count
 
 
-def pack_body(partner, master, one, two, out, lines, *, chunks, rows_step):
-    pitch = 3 * chunks
-    step = pl.program_id(0)
-
-    def group(g, carry):
+def pack_body(partner, master, one, two, out, rows_of, lines, arrived, *, chunks, parts):
+    pitch = 3 * chunks
+    part = master.shape[0] // parts
+    groups = part // SUB
+
+    def fetch(a, ref, p):
+        rows = pl.ds(p * part, part)
+        return pltpu.make_async_copy(ref.at[rows], rows_of.at[a, rows], arrived.at[a, p])
+
+    for p in range(parts):
         for a, ref in enumerate((master, one, two)):
-            for c in range(chunks):
-                tile = ref[pl.ds(pl.multiple_of(g * SUB, SUB), SUB), c * LANES : (c + 1) * LANES]
-                lines[pl.ds(a * chunks + c, SUB, stride=pitch), :] = tile
-        for j in range(SUB):
-            slot = partner[step * rows_step + g * SUB + j] * pitch
-            for i in range(0, pitch, SUB):
-                size = min(SUB, pitch - i)
-                out[pl.ds(slot + i, size), :] = lines[j * pitch + i : j * pitch + i + size, :]
-        return carry
-
-    lax.fori_loop(0, rows_step // SUB, group, 0)
+            fetch(a, ref, p).start()
+
+    for p in range(parts):
+        for a, ref in enumerate((master, one, two)):
+            fetch(a, ref, p).wait()
+
+        def group(g, carry, p=p):
+            row = pl.multiple_of(p * part + g * SUB, SUB)
+            for a in range(3):
+                for c in range(chunks):
+                    tile = rows_of[a, pl.ds(row, SUB), c * LANES : (c + 1) * LANES]
+                    lines[pl.ds(a * chunks + c, SUB, stride=pitch), :] = tile
+            for j in range(SUB):
+                slot = partner[row + j] * pitch
+                for i in range(0, pitch, SUB):
+                    size = min(SUB, pitch - i)
+                    out[pl.ds(slot + i, size), :] = lines[j * pitch + i : j * pitch + i + size, :]
+            return carry
+
+        lax.fori_loop(0, groups, group, 0)
 
 
 def adam_tiles(recv, grad, base, row, c, chunks):
@@ -62,7 +76,9 @@
     return jnp.sum(jnp.where(mine, ids[pl.ds(row, SUB), :], 0), axis=1, keepdims=True)
 
 
-def sums_body(device, partner, ids, recv, grad, out, acc, *, chunks, rows_step):
+def sums_body(
+    device, partner, ids, recv, grad, sums, first_out, second_out, update_out, weights_out, acc, *, chunks, rows_step
+):
     pitch = 3 * chunks
     step = pl.program_id(0)
 
@@ -74,10 +90,16 @@
 
     def group(g, carry):
         row = pl.multiple_of(g * SUB, SUB)
+        kept = pl.multiple_of(step * rows_step + row, SUB)
         update_sq = jnp.zeros((SUB, LANES), jnp.float32)
         weight_sq = jnp.zeros((SUB, LANES), jnp.float32)
         for c in range(chunks):
-            weights, _, _, update = adam_tiles(recv, grad, g * SUB * pitch, row, c, chunks)
+            weights, first, second, update = adam_tiles(recv, grad, g * SUB * pitch, row, c, chunks)
+            cols = slice(c * LANES, (c + 1) * LANES)
+            first_out[pl.ds(row, SUB), cols] = first
+            second_out[pl.ds(row, SUB), cols] = second
+            update_out[pl.ds(kept, SUB), cols] = update
+            weights_out[pl.ds(kept, SUB), cols] = weights
             update_sq += update * update
             weight_sq += weights * weights
         mine = tensor_ids(ids, partner, device[0], row)
@@ -93,24 +115,7 @@
     @pl.when(step == pl.num_programs(0) - 1)
     def _():
         total = jnp.sum(acc[...], axis=0, keepdims=True)
-        out[...] = jnp.broadcast_to(total[None], out.shape)
-
-
-def moments_body(recv, grad, first_out, second_out, update_out, weights_out, *, chunks, rows_step):
-    pitch = 3 * chunks
-
-    def group(g, carry):
-        row = pl.multiple_of(g * SUB, SUB)
-        for c in range(chunks):
-            weights, first, second, update = adam_tiles(recv, grad, g * SUB * pitch, row, c, chunks)
-            cols = slice(c * LANES, (c + 1) * LANES)
-            first_out[pl.ds(row, SUB), cols] = first
-            second_out[pl.ds(row, SUB), cols] = second
-            update_out[pl.ds(row, SUB), cols] = update
-            weights_out[pl.ds(row, SUB), cols] = weights
-        return carry
-
-    lax.fori_loop(0, rows_step // SUB, group, 0)
+        sums[...] = jnp.broadcast_to(total[None], sums.shape)
 
 
 def master_body(device, partner, ids, sums, weights, update, out, *, chunks, rows_step):
@@ -149,39 +154,38 @@
     scalars = pl.BlockSpec(memory_space=pltpu.SMEM)
     array = jax.ShapeDtypeStruct((rows, width), jnp.float32)
 
+    in_hbm = pl.BlockSpec(memory_space=pltpu.HBM)
+    limit = pltpu.CompilerParams(vmem_limit_bytes=16 << 20)
+    parts = 8
     packed = pl.pallas_call(
-        functools.partial(pack_body, **size),
-        grid=(steps,),
-        in_specs=[scalars, row_spec, row_spec, row_spec],
-        out_specs=whole(rows * pitch, LANES),
+        functools.partial(pack_body, chunks=chunks, parts=parts),
+        in_specs=[scalars, in_hbm, in_hbm, in_hbm],
+        out_specs=pl.BlockSpec(memory_space=pltpu.VMEM),
         out_shape=jax.ShapeDtypeStruct((rows * pitch, LANES), jnp.float32),
-        scratch_shapes=[pltpu.VMEM((SUB * pitch, LANES), jnp.float32)],
+        scratch_shapes=[
+            pltpu.VMEM((3, rows, width), jnp.float32),
+            pltpu.VMEM((SUB * pitch, LANES), jnp.float32),
+            pltpu.SemaphoreType.DMA((3, parts)),
+        ],
+        compiler_params=limit,
         name="pack",
-    )(partner, master, moment_one, moment_two)
+    )(*[pltpu.with_memory_space_constraint(v, pltpu.HBM) for v in (partner, master, moment_one, moment_two)])
+    packed, device = lax.optimization_barrier((packed, device))
     sent = packed.reshape(devices, 1, pitch * LANES)
     recv = lax.all_to_all(sent, GRP_SUB, split_axis=0, concat_axis=0, tiled=True)
     recv = recv.reshape(rows * pitch, LANES)
 
-    sums = pl.pallas_call(
+    sums, first, second, update, weights = pl.pallas_call(
         functools.partial(sums_body, **size),
         grid=(steps,),
         in_specs=[scalars, whole(1, devices), ids_spec, recv_spec, row_spec],
-        out_specs=whole(devices, 1, LANES),
-        out_shape=jax.ShapeDtypeStruct((devices, 1, LANES), jnp.float32),
+        out_specs=[whole(devices, 1, LANES), row_spec, row_spec, whole(rows, width), whole(rows, width)],
+        out_shape=[jax.ShapeDtypeStruct((devices, 1, LANES), jnp.float32)] + [array] * 4,
         scratch_shapes=[pltpu.VMEM((SUB, LANES), jnp.float32)],
+        compiler_params=limit,
         name="sums",
     )(device, partner_row, ids, recv, gradient)
     all_sums = lax.all_to_all(sums, GRP_SUB, split_axis=0, concat_axis=0, tiled=True)
-
-    first, second, update, weights = pl.pallas_call(
-        functools.partial(moments_body, **size),
-        grid=(steps,),
-        in_specs=[recv_spec, row_spec],
-        out_specs=[row_spec] * 4,
-        out_shape=[array] * 4,
-        cost_estimate=pl.CostEstimate(flops=30_000_000, bytes_accessed=15_000_000, transcendentals=1_000_000),
-        name="moments",
-    )(recv, gradient)
 
     fresh = pl.pallas_call(
         functools.partial(master_body, **size),
@@ -189,6 +193,7 @@
         in_specs=[scalars, whole(1, devices), ids_spec, whole(devices, 1, LANES), row_spec, row_spec],
         out_specs=row_spec,
         out_shape=array,
+        compiler_params=limit,
         name="fresh",
     )(device, partner_row, ids, all_sums, weights, update)
     return (fresh, first, second)

time: 118 us -> 106 us (0.90)
  blocking collectives: 0 us -> 92.8 us
  waiting for transfers between devices: 69.4 us -> 0 us
  starting transfers between devices: 22 us -> 0 us
  Pallas kernels: 25.3 us -> 12.5 us
    all_to_all x0 -> x2, blocking collectives: none -> 92.8 us  [the longest x1 78.3 us: local(): lax.all_to_all(sent, GRP_SUB, split_axis=0, concat_axis=0, tiled=True)]
    all_to_all x2 -> x0, waiting for transfers between devices: 69.4 us -> none  [the longest x1 66.5 us: local(): lax.all_to_all(sent, GRP_SUB, split_axis=0, concat_axis=0, tiled=True)]
    all_to_all x2 -> x0, starting transfers between devices: 22 us -> none  [the longest x1 11.9 us: local(): lax.all_to_all(sent, GRP_SUB, split_axis=0, concat_axis=0, tiled=True)]
    pallas_call x2 -> x1, Pallas kernels: 12.9 us -> 3.64 us  [local(): pl.pallas_call(functools.partial(pack_body, chunks=chunks, parts=parts),...]
    pallas_call x1, Pallas kernels: 6.25 us -> 4.46 us  [local(): pl.pallas_call(functools.partial(master_body, **size), grid=(steps,), in_...]
    pallas_call x1, Pallas kernels: 6.09 us -> 4.41 us  [local(): pl.pallas_call(functools.partial(sums_body, **size), grid=(steps,), in_sp...]
  transfers between devices with their start and end apart: 2 -> 0, of which waited for: 2 -> 0; matrix products, arithmetic and copies ran while one was open for 0% -> 0% of each run, Pallas kernels for 6% -> 0%
where the time goes in v2:
time: 106 us
  blocking collectives  92.8 us (88%)
  Pallas kernels  12.5 us (12%)
    all_to_all x1, blocking collectives, local(): lax.all_to_all(sent, GRP_SUB, split_axis=0, concat_axis=0, tiled=True)  78.3 us
    all_to_all x1, blocking collectives, local(): lax.all_to_all(sums, GRP_SUB, split_axis=0, concat_axis=0, tiled=True)  14.5 us
    pallas_call x1, Pallas kernels, local(): pl.pallas_call(functools.partial(master_body, **size), grid=(steps,), in_...  4.46 us
    pallas_call x1, Pallas kernels, local(): pl.pallas_call(functools.partial(sums_body, **size), grid=(steps,), in_sp...  4.41 us
    pallas_call x1, Pallas kernels, local(): pl.pallas_call(functools.partial(pack_body, chunks=chunks, parts=parts),...  3.64 us

profile of v2, /device:TPU:1, one launch (start us, length us, event | category | flops | bytes accessed | tf_op | source)
XLA Modules:
  0.0 106.0 jit_solution(11273479916607030796)
XLA Ops:
  0.6 3.6 %pack.1 = f32[10752,128]{1,0:T(8,128)S(1)} custom-call(s32[128]{0:T(128)} %partner.1, f32[128,3584]{1,0:T(8,128)} %master.1, f32[128,3584]{1,0:T(8,128)} %one.1, f32[128,3584]{1,0:T(8,128)} %two.1), custom_call_target="tpu_custom_call" | custom-call | tf_op jit(solution)/shard_map/pack/pallas_call | solution.py:160
  4.3 0.0 copy-start
  4.3 0.0 copy-start.1
  4.3 0.0 copy-start.2
  4.3 78.3 %all_to_all.10 = f32[128,1,10752]{2,1,0:T(1,128)S(1)} all-to-all(f32[128,1,10752]{2,1,0:T(1,128)S(1)} %bitcast.6), channel_id=1, replica_groups=mesh['grp'=32,'sub'=4] {'grp','sub'}, dimensions={0} | all-to-all | bytes 11010048 | tf_op jit(solution)/shard_map/all_to_all | solution.py:175
  82.6 0.0 copy-done
  82.6 0.0 copy-done.1
  82.6 0.0 copy-done.2
  82.6 4.4 %sums.1 = (f32[128,1,128]{2,1,0:T(1,128)S(1)}, f32[128,3584]{1,0:T(8,128)}, f32[128,3584]{1,0:T(8,128)}, f32[128,3584]{1,0:T(8,128)S(1)}, f32[128,3584]{1,0:T(8,128)S(1)}) custom-call(s32[1]{0:T(128)} %bitcast.device, s32[1,128]{1,0:T(1,128)S(1)} %bitcast.9, s32[128,128]{1,0:T(8,128)S(1)} %bitcast.7, f32[10752,128]{1,0:T(8,128)S(1)} %bitcast.5, ...), custom_call_target="tpu_custom_call" | custom-call | tf_op jit(solution)/shard_map/sums/pallas_call | solution.py:178
  87.0 14.5 %all_to_all.11.sums = f32[128,1,128]{2,1,0:T(1,128)S(1)} all-to-all(f32[128,1,128]{2,1,0:T(1,128)S(1)} %get-tuple-element.12), channel_id=1, replica_groups=mesh['grp'=32,'sub'=4] {'grp','sub'}, dimensions={0} | all-to-all | bytes 131072 | tf_op jit(solution)/shard_map/all_to_all | solution.py:188
  101.5 4.5 %fresh.1 = f32[128,3584]{1,0:T(8,128)} custom-call(s32[1]{0:T(128)} %bitcast.device, s32[1,128]{1,0:T(1,128)S(1)} %bitcast.10, s32[128,128]{1,0:T(8,128)S(1)} %bitcast.8, f32[128,1,128]{2,1,0:T(1,128)S(1)} %all_to_all.11.sums, f32[128,3584]{1,0:T(8,128)S(1)} %get-tuple-element.13.weights, f32[128,3584]{1,0:T(8,128)S(1)} %get-tuple-element.14.update), custom_call_target="tpu_custom_call" | custom-call | tf_op jit(solution)/shard_map/fresh/pallas_call | solution.py:190
Async XLA Ops:
  4.3 78.3 %copy-start = (f32[128,3584]{1,0:T(8,128)S(1)}, f32[128,3584]{1,0:T(8,128)}, u32[]{:S(2)}) copy-start(f32[128,3584]{1,0:T(8,128)} %grad.1) | copy-start | bytes 5505028
  4.3 78.3 %copy-start.1 = (s32[16384]{0:T(1024)S(1)}, s32[16384]{0:T(1024)}, u32[]{:S(2)}) copy-start(s32[16384]{0:T(1024)} %param.11) | copy-start | bytes 196612
  4.3 78.3 %copy-start.2 = (s32[128]{0:T(128)S(1)}, s32[128]{0:T(128)}, u32[]{:S(2)}) copy-start(s32[128]{0:T(128)} %partner.1) | copy-start | bytes 1540

commit v3 on v0

v3 whole, which is shorter than its diff:
```python
import functools

import jax
import jax.numpy as jnp
from jax import lax
from jax.experimental import pallas as pl
from jax.experimental.pallas import tpu as pltpu
from jax.sharding import PartitionSpec as P

LAYERS = 8
GRP_SUB = ("grp", "sub")
LANES = 128
SUB = 8
PARTS = 8

beta_one = 0.9
beta_two = 0.999
step_count = 10
adam_eps = 1e-06
trust_eps = 1e-06
learn_rate = 0.05
decay_rate = 0.01
correct_one = 1.0 - beta_one**step_count
correct_two = 1.0 - beta_two**step_count


def pack_body(
    partner_hbm, ids_hbm, master, one, two, out, mine, partner, ids, rows_of, lines, arrived, tables, *, chunks, per_grp
):
    pitch = 3 * chunks
    rows = master.shape[0]
    part = rows // PARTS

    def fetch(a, ref, p):
        span = pl.ds(p * part, part)
        return pltpu.make_async_copy(ref.at[span], rows_of.at[a, span], arrived.at[a, p])

    partner_copy = pltpu.make_async_copy(partner_hbm, partner, tables.at[0])
    ids_copy = pltpu.make_async_copy(ids_hbm, ids, tables.at[1])
    partner_copy.start()
    ids_copy.start()
    for p in range(PARTS):
        for a, ref in enumerate((master, one, two)):
            fetch(a, ref, p).start()

    partner_copy.wait()
    device = lax.axis_index("grp") * per_grp + lax.axis_index("sub")
    rank = jnp.int32(0)
    for n in range(rows):
        rank = jnp.where(partner[n] == device, n, rank)
    lane = lax.broadcasted_iota(jnp.int32, (SUB, LANES), 1)
    ids_copy.wait()
    for g in range(rows // SUB):
        span = slice(g * SUB, (g + 1) * SUB)
        chosen = jnp.sum(jnp.where(lane == rank, ids[span, :], 0), axis=1, keepdims=True)
        mine[span, :] = jnp.broadcast_to(chosen, (SUB, LANES))

    for p in range(PARTS):
        for a, ref in enumerate((master, one, two)):
            fetch(a, ref, p).wait()

        def group(g, carry, p=p):
            row = pl.multiple_of(p * part + g * SUB, SUB)
            for a in range(3):
                for c in range(chunks):
                    tile = rows_of[a, pl.ds(row, SUB), c * LANES : (c + 1) * LANES]
                    lines[pl.ds(a * chunks + c, SUB, stride=pitch), :] = tile
            for j in range(SUB):
                slot = partner[row + j] * pitch
                for i in range(0, pitch, SUB):
                    size = min(SUB, pitch - i)
                    out[pl.ds(slot + i, size), :] = lines[j * pitch + i : j * pitch + i + size, :]
            return carry

        lax.fori_loop(0, part // SUB, group, 0)


def adam_body(recv, grad, mine, first_hbm, second_hbm, sums, update_out, weights_out, first_out, second_out, left, *, chunks):
    pitch = 3 * chunks
    zero = jnp.zeros((SUB, LANES), jnp.float32)
    groups = grad.shape[0] // SUB

    def leave(g):
        span = pl.ds(pl.multiple_of(g * SUB, SUB), SUB)
        return (
            pltpu.make_async_copy(first_out.at[span], first_hbm.at[span], left.at[0, g]),
            pltpu.make_async_copy(second_out.at[span], second_hbm.at[span], left.at[1, g]),
        )

    def group(g, totals):
        row = pl.multiple_of(g * SUB, SUB)
        base = g * SUB * pitch
        update_sq, weight_sq = zero, zero
        for c in range(chunks):
            cols = slice(c * LANES, (c + 1) * LANES)
            weights = recv[pl.ds(base + c, SUB, stride=pitch), :]
            old_one = recv[pl.ds(base + chunks + c, SUB, stride=pitch), :]
            old_two = recv[pl.ds(base + 2 * chunks + c, SUB, stride=pitch), :]
            slope = grad[pl.ds(row, SUB), cols]
            first = beta_one * old_one + (1.0 - beta_one) * slope
            second = beta_two * old_two + (1.0 - beta_two) * slope * slope
            update = (first * (1.0 / correct_one)) / (
                jnp.sqrt(second * (1.0 / correct_two)) + adam_eps
            ) + decay_rate * weights
            first_out[pl.ds(row, SUB), cols] = first
            second_out[pl.ds(row, SUB), cols] = second
            update_out[pl.ds(row, SUB), cols] = update
            weights_out[pl.ds(row, SUB), cols] = weights
            update_sq += update * update
            weight_sq += weights * weights
        for copy in leave(g):
            copy.start()
        tensor = mine[pl.ds(row, SUB), :]
        masks = [tensor == t for t in range(LAYERS)]
        return tuple(
            total + jnp.where(masks[k % LAYERS], update_sq if k < LAYERS else weight_sq, 0.0)
            for k, total in enumerate(totals)
        )

    totals = lax.fori_loop(0, groups, group, (zero,) * (2 * LAYERS))
    lane = lax.broadcasted_iota(jnp.int32, (1, LANES), 1)
    line = jnp.zeros((1, LANES), jnp.float32)
    for k, total in enumerate(totals):
        value = jnp.sum(jnp.sum(total, axis=0, keepdims=True), axis=1, keepdims=True)
        line += jnp.where(lane == k, value, 0.0)
    sums[...] = jnp.broadcast_to(line, sums.shape)
    for g in range(groups):
        for copy in leave(g):
            copy.wait()


def master_body(sums, mine, weights, update, out, fresh, sent):
    rows = weights.shape[0]
    part = rows // PARTS
    total = jnp.broadcast_to(jnp.sum(sums[...], axis=0, keepdims=True), (SUB, LANES))
    weight_sq = pltpu.roll(total, LANES - LAYERS, 1)
    ratio = jnp.sqrt(weight_sq) / (jnp.sqrt(total) + trust_eps)
    lane = lax.broadcasted_iota(jnp.int32, (SUB, LANES), 1)
    scales = [
        jnp.broadcast_to(
            jnp.sum(jnp.where(lane == t, learn_rate * ratio, 0.0), axis=1, keepdims=True), (SUB, LANES)
        )
        for t in range(LAYERS)
    ]

    def leave(p):
        span = pl.ds(p * part, part)
        return pltpu.make_async_copy(fresh.at[span], out.at[span], sent.at[p])

    for p in range(PARTS):
        for g in range(part // SUB):
            span = slice(p * part + g * SUB, p * part + (g + 1) * SUB)
            tensor = mine[span, :]
            scale = scales[0]
            for t in range(1, LAYERS):
                scale = jnp.where(tensor == t, scales[t], scale)
            for c in range(0, weights.shape[1], LANES):
                cols = slice(c, c + LANES)
                fresh[span, cols] = weights[span, cols] - scale * update[span, cols]
        leave(p).start()
    for p in range(PARTS):
        leave(p).wait()


def local(master, moment_one, moment_two, gradient, partner, tensor_of_row):
    rows, width = master.shape
    devices = lax.axis_size(GRP_SUB)
    chunks = width // LANES
    pitch = 3 * chunks
    ids = tensor_of_row.reshape(rows, devices)
    array = jax.ShapeDtypeStruct((rows, width), jnp.float32)
    in_hbm = pl.BlockSpec(memory_space=pltpu.HBM)
    in_vmem = pl.BlockSpec(memory_space=pltpu.VMEM)
    limit = pltpu.CompilerParams(vmem_limit_bytes=16 << 20)
    hbm = lambda v: pltpu.with_memory_space_constraint(v, pltpu.HBM)

    packed, mine = pl.pallas_call(
        functools.partial(pack_body, chunks=chunks, per_grp=lax.axis_size("sub")),
        in_specs=[in_hbm] * 5,
        out_specs=[in_vmem] * 2,
        out_shape=[
            jax.ShapeDtypeStruct((rows * pitch, LANES), jnp.float32),
            jax.ShapeDtypeStruct((rows, LANES), jnp.int32),
        ],
        scratch_shapes=[
            pltpu.SMEM((devices,), jnp.int32),
            pltpu.VMEM((rows, devices), jnp.int32),
            pltpu.VMEM((3, rows, width), jnp.float32),
            pltpu.VMEM((SUB * pitch, LANES), jnp.float32),
            pltpu.SemaphoreType.DMA((3, PARTS)),
            pltpu.SemaphoreType.DMA((2,)),
        ],
        compiler_params=limit,
        name="pack",
    )(hbm(partner), hbm(ids), hbm(master), hbm(moment_one), hbm(moment_two))
    packed, mine = lax.optimization_barrier((packed, mine))
    sent = packed.reshape(devices, 1, pitch * LANES)
    recv = lax.all_to_all(sent, GRP_SUB, split_axis=0, concat_axis=0, tiled=True)
    recv = recv.reshape(rows * pitch, LANES)

    first, second, sums, update, weights = pl.pallas_call(
        functools.partial(adam_body, chunks=chunks),
        in_specs=[in_vmem] * 3,
        out_specs=[in_hbm] * 2 + [in_vmem] * 3,
        out_shape=[array] * 2 + [jax.ShapeDtypeStruct((devices, LANES), jnp.float32)] + [array] * 2,
        scratch_shapes=[pltpu.VMEM((rows, width), jnp.float32)] * 2
        + [pltpu.SemaphoreType.DMA((2, rows // SUB))],
        compiler_params=limit,
        name="adam",
    )(recv, gradient, mine)
    sums = lax.all_to_all(
        sums.reshape(devices, 1, LANES), GRP_SUB, split_axis=0, concat_axis=0, tiled=True
    ).reshape(devices, LANES)

    fresh = pl.pallas_call(
        master_body,
        in_specs=[in_vmem] * 4,
        out_specs=in_hbm,
        out_shape=array,
        scratch_shapes=[pltpu.VMEM((rows, width), jnp.float32), pltpu.SemaphoreType.DMA((PARTS,))],
        compiler_params=limit,
        name="fresh",
    )(sums, mine, weights, update)
    return (fresh, first, second)


def solution(mesh):
    rows = P(GRP_SUB, None)
    return jax.shard_map(
        local,
        mesh=mesh,
        in_specs=(rows, rows, rows, rows, P(), P()),
        out_specs=(rows, rows, rows),
        check_vma=False,
    )
```

time: 170 us -> 102 us (0.60)
  waiting for transfers between devices: 69.1 us -> 0 us
  blocking collectives: 32.1 us -> 92.8 us
  local copies, waits for them, and re-layouts: 25.4 us -> 0.01 us
  starting transfers between devices: 22.9 us -> 0 us
  other arithmetic: 16.6 us -> 0 us
  Pallas kernels: 0 us -> 8.46 us
  between operations: 2.67 us -> 0.66 us
    all_to_all x0 -> x2, blocking collectives: none -> 92.8 us  [the longest x1 78.3 us: local(): lax.all_to_all(sent, GRP_SUB, split_axis=0, concat_axis=0, tiled=True)]
    all_to_all x3 -> x0, waiting for transfers between devices: 69.1 us -> none  [the longest x1 24.3 us: local(): lax.all_to_all(sending[0], GRP_SUB, split_axis=0, concat_axis=0, tiled=True)]
    psum x5 -> x0, blocking collectives: 32.1 us -> none  [one_axis_at_a_time(): return functools.reduce(lax.psum, axes, x)]
    all_to_all x3 -> x0, starting transfers between devices: 22.9 us -> none  [the longest x1 11.9 us: local(): lax.all_to_all(sending[2], GRP_SUB, split_axis=0, concat_axis=0, tiled=True)]
    select_n x3 -> x0, local copies, waits for them, and re-layouts: 12.3 us -> none  [outbound(): return jnp.take(values.reshape(devices, block, width), inverse, axis=0)]
    gather x3 -> x0, local copies, waits for them, and re-layouts: 11.8 us -> none  [outbound(): return jnp.take(values.reshape(devices, block, width), inverse, axis=0)]
    pallas_call x0 -> x3, Pallas kernels: none -> 8.46 us  [the longest x1 3.76 us: local(): pl.pallas_call(functools.partial(pack_body, chunks=chunks, per_grp=lax.ax...]
    reduce_sum x2 -> x0, other arithmetic: 7.95 us -> none  [the longest x1 7.06 us: local(): update_local = tensor_totals(jnp.sum(update * update, axis=1), new_hot)]
  transfers between devices with their start and end apart: 3 -> 0, of which waited for: 3 -> 0; matrix products, arithmetic and copies ran while one was open for 6% -> 0% of each run, Pallas kernels for 0% -> 0%
where the time goes in v3:
time: 102 us
  blocking collectives  92.8 us (91%)
  Pallas kernels  8.46 us (8%)
    all_to_all x1, blocking collectives, local(): lax.all_to_all(sent, GRP_SUB, split_axis=0, concat_axis=0, tiled=True)  78.3 us
    all_to_all x1, blocking collectives, local(): lax.all_to_all(sums.reshape(devices, 1, LANES), GRP_SUB, split_axis=0, co...  14.6 us
    pallas_call x1, Pallas kernels, local(): pl.pallas_call(functools.partial(pack_body, chunks=chunks, per_grp=lax.ax...  3.76 us
    pallas_call x1, Pallas kernels, local(): pl.pallas_call(functools.partial(adam_body, chunks=chunks), in_specs=[in_...  3.2 us

profile of v3, /device:TPU:1, one launch (start us, length us, event | category | flops | bytes accessed | tf_op | source)
XLA Modules:
  0.0 101.9 jit_solution(11586734697208317571)
XLA Ops:
  0.6 3.8 %pack.1 = (f32[10752,128]{1,0:T(8,128)S(1)}, s32[128,128]{1,0:T(8,128)S(1)}) custom-call(s32[128]{0:T(128)} %partner_hbm.1, s32[128,128]{1,0:T(8,128)} %bitcast.11, f32[128,3584]{1,0:T(8,128)} %master.1, f32[128,3584]{1,0:T(8,128)} %one.1, f32[128,3584]{1,0:T(8,128)} %two.1), custom_call_target="tpu_custom_call" | custom-call | tf_op jit(solution)/shard_map/pack/pallas_call | solution.py:177
  4.4 0.0 copy-start
  4.4 78.3 %all_to_all.10 = f32[128,1,10752]{2,1,0:T(1,128)S(1)} all-to-all(f32[128,1,10752]{2,1,0:T(1,128)S(1)} %bitcast.8), channel_id=1, replica_groups=mesh['grp'=32,'sub'=4] {'grp','sub'}, dimensions={0} | all-to-all | bytes 11010048 | tf_op jit(solution)/shard_map/all_to_all | solution.py:198
  82.7 0.0 copy-done
  82.7 3.2 %adam.1 = (f32[128,3584]{1,0:T(8,128)}, f32[128,3584]{1,0:T(8,128)}, f32[128,128]{1,0:T(8,128)S(1)}, f32[128,3584]{1,0:T(8,128)S(1)}, f32[128,3584]{1,0:T(8,128)S(1)}) custom-call(f32[10752,128]{1,0:T(8,128)S(1)} %bitcast.7, f32[128,3584]{1,0:T(8,128)S(1)} %copy-done, s32[128,128]{1,0:T(8,128)S(1)} %get-tuple-element.11.mine), custom_call_target="tpu_custom_call" | custom-call | tf_op jit(solution)/shard_map/adam/pallas_call | solution.py:201
  85.9 14.6 %all_to_all.11 = f32[128,1,128]{2,1,0:T(1,128)S(1)} all-to-all(f32[128,1,128]{2,1,0:T(1,128)S(1)} %bitcast.10), channel_id=1, replica_groups=mesh['grp'=32,'sub'=4] {'grp','sub'}, dimensions={0} | all-to-all | bytes 131072 | tf_op jit(solution)/shard_map/all_to_all | solution.py:211
  100.4 1.5 %fresh.1 = f32[128,3584]{1,0:T(8,128)} custom-call(f32[128,128]{1,0:T(8,128)S(1)} %bitcast.9, s32[128,128]{1,0:T(8,128)S(1)} %get-tuple-element.11.mine, f32[128,3584]{1,0:T(8,128)S(1)} %get-tuple-element.13.weights, f32[128,3584]{1,0:T(8,128)S(1)} %get-tuple-element.14.update), custom_call_target="tpu_custom_call" | custom-call | tf_op jit(solution)/shard_map/fresh/pallas_call | solution.py:215
Async XLA Ops:
  4.4 78.3 %copy-start = (f32[128,3584]{1,0:T(8,128)S(1)}, f32[128,3584]{1,0:T(8,128)}, u32[]{:S(2)}) copy-start(f32[128,3584]{1,0:T(8,128)} %grad.1) | copy-start | bytes 5505028

commit v4 on v3

--- a/solution.py
+++ b/solution.py
@@ -12,6 +12,7 @@
 LANES = 128
 SUB = 8
 PARTS = 8
+SHARES = (7, 5, 3, 1)
 
 beta_one = 0.9
 beta_two = 0.999
@@ -22,6 +23,7 @@
 decay_rate = 0.01
 correct_one = 1.0 - beta_one**step_count
 correct_two = 1.0 - beta_two**step_count
+root_scale = correct_one / correct_two**0.5
 
 
 def pack_body(
@@ -29,17 +31,18 @@
 ):
     pitch = 3 * chunks
     rows = master.shape[0]
-    part = rows // PARTS
+    unit = rows // sum(SHARES)
+    starts = [unit * sum(SHARES[:p]) for p in range(len(SHARES))]
 
     def fetch(a, ref, p):
-        span = pl.ds(p * part, part)
+        span = pl.ds(starts[p], unit * SHARES[p])
         return pltpu.make_async_copy(ref.at[span], rows_of.at[a, span], arrived.at[a, p])
 
     partner_copy = pltpu.make_async_copy(partner_hbm, partner, tables.at[0])
     ids_copy = pltpu.make_async_copy(ids_hbm, ids, tables.at[1])
     partner_copy.start()
     ids_copy.start()
-    for p in range(PARTS):
+    for p in range(len(SHARES)):
         for a, ref in enumerate((master, one, two)):
             fetch(a, ref, p).start()
 
@@ -55,12 +58,12 @@
         chosen = jnp.sum(jnp.where(lane == rank, ids[span, :], 0), axis=1, keepdims=True)
         mine[span, :] = jnp.broadcast_to(chosen, (SUB, LANES))
 
-    for p in range(PARTS):
+    for p in range(len(SHARES)):
         for a, ref in enumerate((master, one, two)):
             fetch(a, ref, p).wait()
 
         def group(g, carry, p=p):
-            row = pl.multiple_of(p * part + g * SUB, SUB)
+            row = pl.multiple_of(starts[p] + g * SUB, SUB)
             for a in range(3):
                 for c in range(chunks):
                     tile = rows_of[a, pl.ds(row, SUB), c * LANES : (c + 1) * LANES]
@@ -72,10 +75,10 @@
                     out[pl.ds(slot + i, size), :] = lines[j * pitch + i : j * pitch + i + size, :]
             return carry
 
-        lax.fori_loop(0, part // SUB, group, 0)
-
-
-def adam_body(recv, grad, mine, first_hbm, second_hbm, sums, update_out, weights_out, first_out, second_out, left, *, chunks):
+        lax.fori_loop(0, unit * SHARES[p] // SUB, group, 0)
+
+
+def adam_body(recv, grad, mine, first_hbm, second_hbm, sums, update_out, first_out, second_out, left, *, chunks):
     pitch = 3 * chunks
     zero = jnp.zeros((SUB, LANES), jnp.float32)
     groups = grad.shape[0] // SUB
@@ -99,13 +102,11 @@
             slope = grad[pl.ds(row, SUB), cols]
             first = beta_one * old_one + (1.0 - beta_one) * slope
             second = beta_two * old_two + (1.0 - beta_two) * slope * slope
-            update = (first * (1.0 / correct_one)) / (
-                jnp.sqrt(second * (1.0 / correct_two)) + adam_eps
-            ) + decay_rate * weights
+            root = second * lax.rsqrt(second)
+            update = first / (root * root_scale + correct_one * adam_eps) + decay_rate * weights
             first_out[pl.ds(row, SUB), cols] = first
             second_out[pl.ds(row, SUB), cols] = second
             update_out[pl.ds(row, SUB), cols] = update
-            weights_out[pl.ds(row, SUB), cols] = weights
             update_sq += update * update
             weight_sq += weights * weights
         for copy in leave(g):
@@ -129,8 +130,9 @@
             copy.wait()
 
 
-def master_body(sums, mine, weights, update, out, fresh, sent):
-    rows = weights.shape[0]
+def master_body(sums, mine, recv, update, out, fresh, sent, *, chunks):
+    rows = update.shape[0]
+    pitch = 3 * chunks
     part = rows // PARTS
     total = jnp.broadcast_to(jnp.sum(sums[...], axis=0, keepdims=True), (SUB, LANES))
     weight_sq = pltpu.roll(total, LANES - LAYERS, 1)
@@ -154,9 +156,10 @@
             scale = scales[0]
             for t in range(1, LAYERS):
                 scale = jnp.where(tensor == t, scales[t], scale)
-            for c in range(0, weights.shape[1], LANES):
-                cols = slice(c, c + LANES)
-                fresh[span, cols] = weights[span, cols] - scale * update[span, cols]
+            for c in range(chunks):
+                cols = slice(c * LANES, (c + 1) * LANES)
+                weights = recv[pl.ds(span.start * pitch + c, SUB, stride=pitch), :]
+                fresh[span, cols] = weights - scale * update[span, cols]
         leave(p).start()
     for p in range(PARTS):
         leave(p).wait()
@@ -187,7 +190,7 @@
             pltpu.VMEM((rows, devices), jnp.int32),
             pltpu.VMEM((3, rows, width), jnp.float32),
             pltpu.VMEM((SUB * pitch, LANES), jnp.float32),
-            pltpu.SemaphoreType.DMA((3, PARTS)),
+            pltpu.SemaphoreType.DMA((3, len(SHARES))),
             pltpu.SemaphoreType.DMA((2,)),
         ],
         compiler_params=limit,
@@ -198,11 +201,11 @@
     recv = lax.all_to_all(sent, GRP_SUB, split_axis=0, concat_axis=0, tiled=True)
     recv = recv.reshape(rows * pitch, LANES)
 
-    first, second, sums, update, weights = pl.pallas_call(
+    first, second, sums, update = pl.pallas_call(
         functools.partial(adam_body, chunks=chunks),
         in_specs=[in_vmem] * 3,
-        out_specs=[in_hbm] * 2 + [in_vmem] * 3,
-        out_shape=[array] * 2 + [jax.ShapeDtypeStruct((devices, LANES), jnp.float32)] + [array] * 2,
+        out_specs=[in_hbm] * 2 + [in_vmem] * 2,
+        out_shape=[array] * 2 + [jax.ShapeDtypeStruct((devices, LANES), jnp.float32), array],
         scratch_shapes=[pltpu.VMEM((rows, width), jnp.float32)] * 2
         + [pltpu.SemaphoreType.DMA((2, rows // SUB))],
         compiler_params=limit,
@@ -213,14 +216,14 @@
     ).reshape(devices, LANES)
 
     fresh = pl.pallas_call(
-        master_body,
+        functools.partial(master_body, chunks=chunks),
         in_specs=[in_vmem] * 4,
         out_specs=in_hbm,
         out_shape=array,
         scratch_shapes=[pltpu.VMEM((rows, width), jnp.float32), pltpu.SemaphoreType.DMA((PARTS,))],
         compiler_params=limit,
         name="fresh",
-    )(sums, mine, weights, update)
+    )(sums, mine, recv, update)
     return (fresh, first, second)
 
 

time: 102 us -> 101 us (level)
  no operation moved by 1% of the time
where the time goes in v4:
time: 101 us
  blocking collectives  92.8 us (92%)
  Pallas kernels  7.46 us (7%)
    all_to_all x1, blocking collectives, local(): lax.all_to_all(sent, GRP_SUB, split_axis=0, concat_axis=0, tiled=True)  78.3 us
    all_to_all x1, blocking collectives, local(): lax.all_to_all(sums.reshape(devices, 1, LANES), GRP_SUB, split_axis=0, co...  14.6 us
    pallas_call x1, Pallas kernels, local(): pl.pallas_call(functools.partial(pack_body, chunks=chunks, per_grp=lax.ax...  3.54 us
    pallas_call x1, Pallas kernels, local(): pl.pallas_call(functools.partial(adam_body, chunks=chunks), in_specs=[in_...  2.42 us

profile of v4, /device:TPU:1, one launch (start us, length us, event | category | flops | bytes accessed | tf_op | source)
XLA Modules:
  0.0 100.9 jit_solution(12044076871966182638)
XLA Ops:
  0.6 3.5 %pack.1 = (f32[10752,128]{1,0:T(8,128)S(1)}, s32[128,128]{1,0:T(8,128)S(1)}) custom-call(s32[128]{0:T(128)} %partner_hbm.1, s32[128,128]{1,0:T(8,128)} %bitcast.12, f32[128,3584]{1,0:T(8,128)} %master.1, f32[128,3584]{1,0:T(8,128)} %one.1, f32[128,3584]{1,0:T(8,128)} %two.1), custom_call_target="tpu_custom_call" | custom-call | tf_op jit(solution)/shard_map/pack/pallas_call | solution.py:180
  4.2 0.0 copy-start
  4.2 78.3 %all_to_all.10 = f32[128,1,10752]{2,1,0:T(1,128)S(1)} all-to-all(f32[128,1,10752]{2,1,0:T(1,128)S(1)} %bitcast.9), channel_id=1, replica_groups=mesh['grp'=32,'sub'=4] {'grp','sub'}, dimensions={0} | all-to-all | bytes 11010048 | tf_op jit(solution)/shard_map/all_to_all | solution.py:201
  82.4 0.0 copy-done
  82.4 2.4 %adam.1 = (f32[128,3584]{1,0:T(8,128)}, f32[128,3584]{1,0:T(8,128)}, f32[128,128]{1,0:T(8,128)S(1)}, f32[128,3584]{1,0:T(8,128)S(1)}) custom-call(f32[10752,128]{1,0:T(8,128)S(1)} %bitcast.7, f32[128,3584]{1,0:T(8,128)S(1)} %copy-done, s32[128,128]{1,0:T(8,128)S(1)} %get-tuple-element.10.mine), custom_call_target="tpu_custom_call" | custom-call | tf_op jit(solution)/shard_map/adam/pallas_call | solution.py:204
  84.9 14.6 %all_to_all.11 = f32[128,1,128]{2,1,0:T(1,128)S(1)} all-to-all(f32[128,1,128]{2,1,0:T(1,128)S(1)} %bitcast.11), channel_id=1, replica_groups=mesh['grp'=32,'sub'=4] {'grp','sub'}, dimensions={0} | all-to-all | bytes 131072 | tf_op jit(solution)/shard_map/all_to_all | solution.py:214
  99.4 1.5 %fresh.1 = f32[128,3584]{1,0:T(8,128)} custom-call(f32[128,128]{1,0:T(8,128)S(1)} %bitcast.10, s32[128,128]{1,0:T(8,128)S(1)} %get-tuple-element.10.mine, f32[10752,128]{1,0:T(8,128)S(1)} %bitcast.8, f32[128,3584]{1,0:T(8,128)S(1)} %get-tuple-element.12.update), custom_call_target="tpu_custom_call" | custom-call | tf_op jit(solution)/shard_map/fresh/pallas_call | solution.py:218
Async XLA Ops:
  4.2 78.3 %copy-start = (f32[128,3584]{1,0:T(8,128)S(1)}, f32[128,3584]{1,0:T(8,128)}, u32[]{:S(2)}) copy-start(f32[128,3584]{1,0:T(8,128)} %grad.1) | copy-start | bytes 5505028

commit v5 on v4

--- a/solution.py
+++ b/solution.py
@@ -12,7 +12,7 @@
 LANES = 128
 SUB = 8
 PARTS = 8
-SHARES = (7, 5, 3, 1)
+SHARES = (8, 8)
 
 beta_one = 0.9
 beta_two = 0.999

time: 101 us -> 101 us (level)
  no operation moved by 1% of the time
where the time goes in v5:
time: 101 us
  blocking collectives  92.8 us (92%)
  Pallas kernels  7.16 us (7%)
    all_to_all x1, blocking collectives, local(): lax.all_to_all(sent, GRP_SUB, split_axis=0, concat_axis=0, tiled=True)  78.3 us
    all_to_all x1, blocking collectives, local(): lax.all_to_all(sums.reshape(devices, 1, LANES), GRP_SUB, split_axis=0, co...  14.6 us
    pallas_call x1, Pallas kernels, local(): pl.pallas_call(functools.partial(pack_body, chunks=chunks, per_grp=lax.ax...  3.25 us
    pallas_call x1, Pallas kernels, local(): pl.pallas_call(functools.partial(adam_body, chunks=chunks), in_specs=[in_...  2.42 us

profile of v5, /device:TPU:1, one launch (start us, length us, event | category | flops | bytes accessed | tf_op | source)
XLA Modules:
  0.0 100.6 jit_solution(7893476244265956407)
XLA Ops:
  0.6 3.2 %pack.1 = (f32[10752,128]{1,0:T(8,128)S(1)}, s32[128,128]{1,0:T(8,128)S(1)}) custom-call(s32[128]{0:T(128)} %partner_hbm.1, s32[128,128]{1,0:T(8,128)} %bitcast.12, f32[128,3584]{1,0:T(8,128)} %master.1, f32[128,3584]{1,0:T(8,128)} %one.1, f32[128,3584]{1,0:T(8,128)} %two.1), custom_call_target="tpu_custom_call" | custom-call | tf_op jit(solution)/shard_map/pack/pallas_call | solution.py:180
  3.9 0.0 copy-start
  3.9 78.3 %all_to_all.10 = f32[128,1,10752]{2,1,0:T(1,128)S(1)} all-to-all(f32[128,1,10752]{2,1,0:T(1,128)S(1)} %bitcast.9), channel_id=1, replica_groups=mesh['grp'=32,'sub'=4] {'grp','sub'}, dimensions={0} | all-to-all | bytes 11010048 | tf_op jit(solution)/shard_map/all_to_all | solution.py:201
  82.1 0.0 copy-done
  82.2 2.4 %adam.1 = (f32[128,3584]{1,0:T(8,128)}, f32[128,3584]{1,0:T(8,128)}, f32[128,128]{1,0:T(8,128)S(1)}, f32[128,3584]{1,0:T(8,128)S(1)}) custom-call(f32[10752,128]{1,0:T(8,128)S(1)} %bitcast.7, f32[128,3584]{1,0:T(8,128)S(1)} %copy-done, s32[128,128]{1,0:T(8,128)S(1)} %get-tuple-element.10.mine), custom_call_target="tpu_custom_call" | custom-call | tf_op jit(solution)/shard_map/adam/pallas_call | solution.py:204
  84.6 14.6 %all_to_all.11 = f32[128,1,128]{2,1,0:T(1,128)S(1)} all-to-all(f32[128,1,128]{2,1,0:T(1,128)S(1)} %bitcast.11), channel_id=1, replica_groups=mesh['grp'=32,'sub'=4] {'grp','sub'}, dimensions={0} | all-to-all | bytes 131072 | tf_op jit(solution)/shard_map/all_to_all | solution.py:214
  99.1 1.5 %fresh.1 = f32[128,3584]{1,0:T(8,128)} custom-call(f32[128,128]{1,0:T(8,128)S(1)} %bitcast.10, s32[128,128]{1,0:T(8,128)S(1)} %get-tuple-element.10.mine, f32[10752,128]{1,0:T(8,128)S(1)} %bitcast.8, f32[128,3584]{1,0:T(8,128)S(1)} %get-tuple-element.12.update), custom_call_target="tpu_custom_call" | custom-call | tf_op jit(solution)/shard_map/fresh/pallas_call | solution.py:218
Async XLA Ops:
  3.9 78.3 %copy-start = (f32[128,3584]{1,0:T(8,128)S(1)}, f32[128,3584]{1,0:T(8,128)}, u32[]{:S(2)}) copy-start(f32[128,3584]{1,0:T(8,128)} %grad.1) | copy-start | bytes 5505028

commit v6 on v5

--- a/solution.py
+++ b/solution.py
@@ -12,7 +12,8 @@
 LANES = 128
 SUB = 8
 PARTS = 8
-SHARES = (8, 8)
+SHARES = (8, 5, 3)
+URGENCY = (0, 1, 1)
 
 beta_one = 0.9
 beta_two = 0.999
@@ -44,7 +45,7 @@
     ids_copy.start()
     for p in range(len(SHARES)):
         for a, ref in enumerate((master, one, two)):
-            fetch(a, ref, p).start()
+            fetch(a, ref, p).start(priority=URGENCY[p])
 
     partner_copy.wait()
     device = lax.axis_index("grp") * per_grp + lax.axis_index("sub")

time: 101 us -> 100 us (0.990)
  no operation moved by 1% of the time
where the time goes in v6:
time: 100 us
  blocking collectives  92.8 us (93%)
  Pallas kernels  6.72 us (7%)
    all_to_all x1, blocking collectives, local(): lax.all_to_all(sent, GRP_SUB, split_axis=0, concat_axis=0, tiled=True)  78.3 us
    all_to_all x1, blocking collectives, local(): lax.all_to_all(sums.reshape(devices, 1, LANES), GRP_SUB, split_axis=0, co...  14.6 us
    pallas_call x1, Pallas kernels, local(): pl.pallas_call(functools.partial(pack_body, chunks=chunks, per_grp=lax.ax...  2.8 us
    pallas_call x1, Pallas kernels, local(): pl.pallas_call(functools.partial(adam_body, chunks=chunks), in_specs=[in_...  2.42 us

profile of v6, /device:TPU:1, one launch (start us, length us, event | category | flops | bytes accessed | tf_op | source)
XLA Modules:
  0.0 100.2 jit_solution(5206367656469060020)
XLA Ops:
  0.6 2.8 %pack.1 = (f32[10752,128]{1,0:T(8,128)S(1)}, s32[128,128]{1,0:T(8,128)S(1)}) custom-call(s32[128]{0:T(128)} %partner_hbm.1, s32[128,128]{1,0:T(8,128)} %bitcast.12, f32[128,3584]{1,0:T(8,128)} %master.1, f32[128,3584]{1,0:T(8,128)} %one.1, f32[128,3584]{1,0:T(8,128)} %two.1), custom_call_target="tpu_custom_call" | custom-call | tf_op jit(solution)/shard_map/pack/pallas_call | solution.py:181
  3.4 0.0 copy-start
  3.5 78.3 %all_to_all.10 = f32[128,1,10752]{2,1,0:T(1,128)S(1)} all-to-all(f32[128,1,10752]{2,1,0:T(1,128)S(1)} %bitcast.9), channel_id=1, replica_groups=mesh['grp'=32,'sub'=4] {'grp','sub'}, dimensions={0} | all-to-all | bytes 11010048 | tf_op jit(solution)/shard_map/all_to_all | solution.py:202
  81.7 0.0 copy-done
  81.7 2.4 %adam.1 = (f32[128,3584]{1,0:T(8,128)}, f32[128,3584]{1,0:T(8,128)}, f32[128,128]{1,0:T(8,128)S(1)}, f32[128,3584]{1,0:T(8,128)S(1)}) custom-call(f32[10752,128]{1,0:T(8,128)S(1)} %bitcast.7, f32[128,3584]{1,0:T(8,128)S(1)} %copy-done, s32[128,128]{1,0:T(8,128)S(1)} %get-tuple-element.10.mine), custom_call_target="tpu_custom_call" | custom-call | tf_op jit(solution)/shard_map/adam/pallas_call | solution.py:205
  84.1 14.6 %all_to_all.11 = f32[128,1,128]{2,1,0:T(1,128)S(1)} all-to-all(f32[128,1,128]{2,1,0:T(1,128)S(1)} %bitcast.11), channel_id=1, replica_groups=mesh['grp'=32,'sub'=4] {'grp','sub'}, dimensions={0} | all-to-all | bytes 131072 | tf_op jit(solution)/shard_map/all_to_all | solution.py:215
  98.7 1.5 %fresh.1 = f32[128,3584]{1,0:T(8,128)} custom-call(f32[128,128]{1,0:T(8,128)S(1)} %bitcast.10, s32[128,128]{1,0:T(8,128)S(1)} %get-tuple-element.10.mine, f32[10752,128]{1,0:T(8,128)S(1)} %bitcast.8, f32[128,3584]{1,0:T(8,128)S(1)} %get-tuple-element.12.update), custom_call_target="tpu_custom_call" | custom-call | tf_op jit(solution)/shard_map/fresh/pallas_call | solution.py:219
Async XLA Ops:
  3.4 78.3 %copy-start = (f32[128,3584]{1,0:T(8,128)S(1)}, f32[128,3584]{1,0:T(8,128)}, u32[]{:S(2)}) copy-start(f32[128,3584]{1,0:T(8,128)} %grad.1) | copy-start | bytes 5505028

commit v7 on v6

--- a/solution.py
+++ b/solution.py
@@ -14,6 +14,7 @@
 PARTS = 8
 SHARES = (8, 5, 3)
 URGENCY = (0, 1, 1)
+LATE = 6
 
 beta_one = 0.9
 beta_two = 0.999
@@ -79,10 +80,11 @@
         lax.fori_loop(0, unit * SHARES[p] // SUB, group, 0)
 
 
-def adam_body(recv, grad, mine, first_hbm, second_hbm, sums, update_out, first_out, second_out, left, *, chunks):
+def adam_body(recv, grad, mine, first_hbm, second_hbm, sums, update_out, first_late, second_late, first_out, second_out, left, *, chunks):
     pitch = 3 * chunks
     zero = jnp.zeros((SUB, LANES), jnp.float32)
     groups = grad.shape[0] // SUB
+    early = groups - LATE
 
     def leave(g):
         span = pl.ds(pl.multiple_of(g * SUB, SUB), SUB)
@@ -91,8 +93,9 @@
             pltpu.make_async_copy(second_out.at[span], second_hbm.at[span], left.at[1, g]),
         )
 
-    def group(g, totals):
+    def group(g, totals, late):
         row = pl.multiple_of(g * SUB, SUB)
+        kept = pl.multiple_of((g - early) * SUB, SUB) if late else row
         base = g * SUB * pitch
         update_sq, weight_sq = zero, zero
         for c in range(chunks):
@@ -105,13 +108,14 @@
             second = beta_two * old_two + (1.0 - beta_two) * slope * slope
             root = second * lax.rsqrt(second)
             update = first / (root * root_scale + correct_one * adam_eps) + decay_rate * weights
-            first_out[pl.ds(row, SUB), cols] = first
-            second_out[pl.ds(row, SUB), cols] = second
+            (first_late if late else first_out)[pl.ds(kept, SUB), cols] = first
+            (second_late if late else second_out)[pl.ds(kept, SUB), cols] = second
             update_out[pl.ds(row, SUB), cols] = update
             update_sq += update * update
             weight_sq += weights * weights
-        for copy in leave(g):
-            copy.start()
+        if not late:
+            for copy in leave(g):
+                copy.start()
         tensor = mine[pl.ds(row, SUB), :]
         masks = [tensor == t for t in range(LAYERS)]
         return tuple(
@@ -119,20 +123,45 @@
             for k, total in enumerate(totals)
         )
 
-    totals = lax.fori_loop(0, groups, group, (zero,) * (2 * LAYERS))
+    totals = lax.fori_loop(0, early, functools.partial(group, late=False), (zero,) * (2 * LAYERS))
+    totals = lax.fori_loop(early, groups, functools.partial(group, late=True), totals)
     lane = lax.broadcasted_iota(jnp.int32, (1, LANES), 1)
     line = jnp.zeros((1, LANES), jnp.float32)
     for k, total in enumerate(totals):
         value = jnp.sum(jnp.sum(total, axis=0, keepdims=True), axis=1, keepdims=True)
         line += jnp.where(lane == k, value, 0.0)
     sums[...] = jnp.broadcast_to(line, sums.shape)
-    for g in range(groups):
+    for g in range(early):
         for copy in leave(g):
             copy.wait()
 
 
-def master_body(sums, mine, recv, update, out, fresh, sent, *, chunks):
+def master_body(
+    sums,
+    mine,
+    recv,
+    update,
+    first_late,
+    second_late,
+    first_in,
+    second_in,
+    out,
+    first_out,
+    second_out,
+    fresh,
+    sent,
+    late,
+    *,
+    chunks,
+):
     rows = update.shape[0]
+    rest = pl.ds(rows - LATE * SUB, LATE * SUB)
+    late_copies = [
+        pltpu.make_async_copy(source, whole.at[rest], late.at[k])
+        for k, (source, whole) in enumerate(((first_late, first_out), (second_late, second_out)))
+    ]
+    for copy in late_copies:
+        copy.start()
     pitch = 3 * chunks
     part = rows // PARTS
     total = jnp.broadcast_to(jnp.sum(sums[...], axis=0, keepdims=True), (SUB, LANES))
@@ -162,6 +191,8 @@
                 weights = recv[pl.ds(span.start * pitch + c, SUB, stride=pitch), :]
                 fresh[span, cols] = weights - scale * update[span, cols]
         leave(p).start()
+    for copy in late_copies:
+        copy.wait()
     for p in range(PARTS):
         leave(p).wait()
 
@@ -202,13 +233,14 @@
     recv = lax.all_to_all(sent, GRP_SUB, split_axis=0, concat_axis=0, tiled=True)
     recv = recv.reshape(rows * pitch, LANES)
 
-    first, second, sums, update = pl.pallas_call(
+    late = jax.ShapeDtypeStruct((LATE * SUB, width), jnp.float32)
+    first, second, sums, update, first_late, second_late = pl.pallas_call(
         functools.partial(adam_body, chunks=chunks),
         in_specs=[in_vmem] * 3,
-        out_specs=[in_hbm] * 2 + [in_vmem] * 2,
-        out_shape=[array] * 2 + [jax.ShapeDtypeStruct((devices, LANES), jnp.float32), array],
-        scratch_shapes=[pltpu.VMEM((rows, width), jnp.float32)] * 2
-        + [pltpu.SemaphoreType.DMA((2, rows // SUB))],
+        out_specs=[in_hbm] * 2 + [in_vmem] * 4,
+        out_shape=[array] * 2 + [jax.ShapeDtypeStruct((devices, LANES), jnp.float32), array] + [late] * 2,
+        scratch_shapes=[pltpu.VMEM((rows - LATE * SUB, width), jnp.float32)] * 2
+        + [pltpu.SemaphoreType.DMA((2, rows // SUB - LATE))],
         compiler_params=limit,
         name="adam",
     )(recv, gradient, mine)
@@ -216,15 +248,20 @@
         sums.reshape(devices, 1, LANES), GRP_SUB, split_axis=0, concat_axis=0, tiled=True
     ).reshape(devices, LANES)
 
-    fresh = pl.pallas_call(
+    fresh, first, second = pl.pallas_call(
         functools.partial(master_body, chunks=chunks),
-        in_specs=[in_vmem] * 4,
-        out_specs=in_hbm,
-        out_shape=array,
-        scratch_shapes=[pltpu.VMEM((rows, width), jnp.float32), pltpu.SemaphoreType.DMA((PARTS,))],
+        in_specs=[in_vmem] * 6 + [in_hbm] * 2,
+        out_specs=[in_hbm] * 3,
+        out_shape=[array] * 3,
+        input_output_aliases={6: 1, 7: 2},
+        scratch_shapes=[
+            pltpu.VMEM((rows, width), jnp.float32),
+            pltpu.SemaphoreType.DMA((PARTS,)),
+            pltpu.SemaphoreType.DMA((2,)),
+        ],
         compiler_params=limit,
         name="fresh",
-    )(sums, mine, recv, update)
+    )(sums, mine, recv, update, first_late, second_late, hbm(first), hbm(second))
     return (fresh, first, second)
 
 

time: 100 us -> 100 us (level)
  no operation moved by 1% of the time
where the time goes in v7:
time: 100 us
  blocking collectives  92.8 us (93%)
  Pallas kernels  6.56 us (7%)
    all_to_all x1, blocking collectives, local(): lax.all_to_all(sent, GRP_SUB, split_axis=0, concat_axis=0, tiled=True)  78.3 us
    all_to_all x1, blocking collectives, local(): lax.all_to_all(sums.reshape(devices, 1, LANES), GRP_SUB, split_axis=0, co...  14.6 us
    pallas_call x1, Pallas kernels, local(): pl.pallas_call(functools.partial(pack_body, chunks=chunks, per_grp=lax.ax...  2.8 us

profile of v7, /device:TPU:1, one launch (start us, length us, event | category | flops | bytes accessed | tf_op | source)
XLA Modules:
  0.0 100.0 jit_solution(11407912875181707646)
XLA Ops:
  0.6 2.8 %pack.1 = (f32[10752,128]{1,0:T(8,128)S(1)}, s32[128,128]{1,0:T(8,128)S(1)}) custom-call(s32[128]{0:T(128)} %partner_hbm.1, s32[128,128]{1,0:T(8,128)} %bitcast.12, f32[128,3584]{1,0:T(8,128)} %master.1, f32[128,3584]{1,0:T(8,128)} %one.1, f32[128,3584]{1,0:T(8,128)} %two.1), custom_call_target="tpu_custom_call" | custom-call | tf_op jit(solution)/shard_map/pack/pallas_call | solution.py:212
  3.4 0.0 copy-start
  3.5 78.3 %all_to_all.10 = f32[128,1,10752]{2,1,0:T(1,128)S(1)} all-to-all(f32[128,1,10752]{2,1,0:T(1,128)S(1)} %bitcast.9), channel_id=1, replica_groups=mesh['grp'=32,'sub'=4] {'grp','sub'}, dimensions={0} | all-to-all | bytes 11010048 | tf_op jit(solution)/shard_map/all_to_all | solution.py:233
  81.7 0.0 copy-done
  81.7 1.8 %adam.1 = (f32[128,3584]{1,0:T(8,128)}, f32[128,3584]{1,0:T(8,128)}, f32[128,128]{1,0:T(8,128)S(1)}, f32[128,3584]{1,0:T(8,128)S(1)}, f32[48,3584]{1,0:T(8,128)S(1)}, /*index=5*/f32[48,3584]{1,0:T(8,128)S(1)}) custom-call(f32[10752,128]{1,0:T(8,128)S(1)} %bitcast.7, f32[128,3584]{1,0:T(8,128)S(1)} %copy-done, s32[128,128]{1,0:T(8,128)S(1)} %get-tuple-element.12.mine), custom_call_target="tpu_custom_call" | custom-call | tf_op jit(solution)/shard_map/adam/pallas_call | solution.py:237
  83.5 14.6 %all_to_all.11 = f32[128,1,128]{2,1,0:T(1,128)S(1)} all-to-all(f32[128,1,128]{2,1,0:T(1,128)S(1)} %bitcast.11), channel_id=1, replica_groups=mesh['grp'=32,'sub'=4] {'grp','sub'}, dimensions={0} | all-to-all | bytes 131072 | tf_op jit(solution)/shard_map/all_to_all | solution.py:247
  98.1 2.0 %fresh.1 = (f32[128,3584]{1,0:T(8,128)}, f32[128,3584]{1,0:T(8,128)}, f32[128,3584]{1,0:T(8,128)}) custom-call(f32[128,128]{1,0:T(8,128)S(1)} %bitcast.10, s32[128,128]{1,0:T(8,128)S(1)} %get-tuple-element.12.mine, f32[10752,128]{1,0:T(8,128)S(1)} %bitcast.8, ...), custom_call_target="tpu_custom_call", output_to_operand_aliasing={{1}: (6, {}), {2}: (7, {})} | custom-call | tf_op jit(solution)/shard_map/fresh/pallas_call | solution.py:251
Async XLA Ops:
  3.4 78.3 %copy-start = (f32[128,3584]{1,0:T(8,128)S(1)}, f32[128,3584]{1,0:T(8,128)}, u32[]{:S(2)}) copy-start(f32[128,3584]{1,0:T(8,128)} %grad.1) | copy-start | bytes 5505028

commit v8 on v7

--- a/solution.py
+++ b/solution.py
@@ -125,11 +125,16 @@
 
     totals = lax.fori_loop(0, early, functools.partial(group, late=False), (zero,) * (2 * LAYERS))
     totals = lax.fori_loop(early, groups, functools.partial(group, late=True), totals)
-    lane = lax.broadcasted_iota(jnp.int32, (1, LANES), 1)
-    line = jnp.zeros((1, LANES), jnp.float32)
-    for k, total in enumerate(totals):
-        value = jnp.sum(jnp.sum(total, axis=0, keepdims=True), axis=1, keepdims=True)
-        line += jnp.where(lane == k, value, 0.0)
+    lane = lax.broadcasted_iota(jnp.int32, (SUB, LANES), 1)
+    sub = lax.broadcasted_iota(jnp.int32, (SUB, LANES), 0)
+    placed = zero
+    for first_lane in (0, LAYERS):
+        stacked = zero
+        for t in range(LAYERS):
+            stacked = jnp.where(sub == t, jnp.sum(totals[first_lane + t], axis=0, keepdims=True), stacked)
+        values = jnp.sum(stacked, axis=1, keepdims=True)
+        placed += jnp.where(lane == sub + first_lane, values, 0.0)
+    line = jnp.sum(placed, axis=0, keepdims=True)
     sums[...] = jnp.broadcast_to(line, sums.shape)
     for g in range(early):
         for copy in leave(g):

time: 100 us -> 100 us (level)
  no operation moved by 1% of the time
where the time goes in v8:
time: 100 us
  blocking collectives  92.8 us (93%)
  Pallas kernels  6.57 us (7%)
    all_to_all x1, blocking collectives, local(): lax.all_to_all(sent, GRP_SUB, split_axis=0, concat_axis=0, tiled=True)  78.3 us
    all_to_all x1, blocking collectives, local(): lax.all_to_all(sums.reshape(devices, 1, LANES), GRP_SUB, split_axis=0, co...  14.6 us
    pallas_call x1, Pallas kernels, local(): pl.pallas_call(functools.partial(pack_body, chunks=chunks, per_grp=lax.ax...  2.8 us

profile of v8, /device:TPU:1, one launch (start us, length us, event | category | flops | bytes accessed | tf_op | source)
XLA Modules:
  0.0 100.0 jit_solution(14132400868204481444)
XLA Ops:
  0.6 2.8 %pack.1 = (f32[10752,128]{1,0:T(8,128)S(1)}, s32[128,128]{1,0:T(8,128)S(1)}) custom-call(s32[128]{0:T(128)} %partner_hbm.1, s32[128,128]{1,0:T(8,128)} %bitcast.12, f32[128,3584]{1,0:T(8,128)} %master.1, f32[128,3584]{1,0:T(8,128)} %one.1, f32[128,3584]{1,0:T(8,128)} %two.1), custom_call_target="tpu_custom_call" | custom-call | tf_op jit(solution)/shard_map/pack/pallas_call | solution.py:217
  3.4 0.0 copy-start
  3.5 78.3 %all_to_all.10 = f32[128,1,10752]{2,1,0:T(1,128)S(1)} all-to-all(f32[128,1,10752]{2,1,0:T(1,128)S(1)} %bitcast.9), channel_id=1, replica_groups=mesh['grp'=32,'sub'=4] {'grp','sub'}, dimensions={0} | all-to-all | bytes 11010048 | tf_op jit(solution)/shard_map/all_to_all | solution.py:238
  81.7 0.0 copy-done
  81.7 1.8 %adam.1 = (f32[128,3584]{1,0:T(8,128)}, f32[128,3584]{1,0:T(8,128)}, f32[128,128]{1,0:T(8,128)S(1)}, f32[128,3584]{1,0:T(8,128)S(1)}, f32[48,3584]{1,0:T(8,128)S(1)}, /*index=5*/f32[48,3584]{1,0:T(8,128)S(1)}) custom-call(f32[10752,128]{1,0:T(8,128)S(1)} %bitcast.7, f32[128,3584]{1,0:T(8,128)S(1)} %copy-done, s32[128,128]{1,0:T(8,128)S(1)} %get-tuple-element.12.mine), custom_call_target="tpu_custom_call" | custom-call | tf_op jit(solution)/shard_map/adam/pallas_call | solution.py:242
  83.5 14.6 %all_to_all.11 = f32[128,1,128]{2,1,0:T(1,128)S(1)} all-to-all(f32[128,1,128]{2,1,0:T(1,128)S(1)} %bitcast.11), channel_id=1, replica_groups=mesh['grp'=32,'sub'=4] {'grp','sub'}, dimensions={0} | all-to-all | bytes 131072 | tf_op jit(solution)/shard_map/all_to_all | solution.py:252
  98.1 2.0 %fresh.1 = (f32[128,3584]{1,0:T(8,128)}, f32[128,3584]{1,0:T(8,128)}, f32[128,3584]{1,0:T(8,128)}) custom-call(f32[128,128]{1,0:T(8,128)S(1)} %bitcast.10, s32[128,128]{1,0:T(8,128)S(1)} %get-tuple-element.12.mine, f32[10752,128]{1,0:T(8,128)S(1)} %bitcast.8, ...), custom_call_target="tpu_custom_call", output_to_operand_aliasing={{1}: (6, {}), {2}: (7, {})} | custom-call | tf_op jit(solution)/shard_map/fresh/pallas_call | solution.py:256
Async XLA Ops:
  3.4 78.3 %copy-start = (f32[128,3584]{1,0:T(8,128)S(1)}, f32[128,3584]{1,0:T(8,128)}, u32[]{:S(2)}) copy-start(f32[128,3584]{1,0:T(8,128)} %grad.1) | copy-start | bytes 5505028
